TPU v7x, 256 devices: a whole 4x4x8 slice. The times are simulated.
256 devices in a mesh: ha: 16 (over z, core), wa: 8 (over y, x_lo), ba: 2 (over x_hi).
Axes of the slice: x: 4 (x_hi: 2, x_lo: 2; x = x_hi * 2 + x_lo), y: 4, z: 8, core: 2. Of those that a mesh axis runs over, the one named last changes fastest.
Arguments:
- tokens: bfloat16 [2, 256, 256, 384], P('ba', 'ha', 'wa'), may hold values from -6 to 6
- cotangent: bfloat16 [2, 256, 256, 384], P('ba', 'ha', 'wa'), may hold values from -6 to 6
- w_qkv: bfloat16 [384, 1152], replicated, may hold values from -0.20412415 to 0.20412415
- w_proj: bfloat16 [384, 384], replicated, may hold values from -0.3125 to 0.3125
- table_logits: float32 [12, 225], replicated, may hold values from -6 to 6
- logit_scale: float32 [12], replicated, may hold values from 1 to 5.5
- gain: float32 [384], replicated, may hold values from 0.5 to 1.5
Outputs:
- d_tokens: bfloat16 [2, 256, 256, 384], P('ba', 'ha', 'wa')
- d_wqkv: float32 [384, 1152], P(None, 'ba')
- d_wproj: float32 [384, 384], P(None, 'ba')
- d_table: float32 [12, 225], replicated
- d_scale: float32 [12], replicated
- d_gain: float32 [384], replicated
All inputs are finite; a program needn't handle non-finite values.
Results may differ from a plain program's by a relative error of at most 0.01.
The roundings to bfloat16 on the way count: a program that leaves them out, or rounds other values in their place, can miss the bound.
Values may be sent and summed in bfloat16 or wider, within the bound.
A program may use at most 64 MiB of HBM per device.

v0:
```python
import math

import jax
import jax.numpy as jnp
from jax import lax
from jax.sharding import Mesh
from jax.sharding import PartitionSpec as P

WIN = 8
HA = ("ha_0", "ha_1")
WA = ("wa_0", "wa_1")


EPS_NORM = 1e-05
MASK_FILL = -100.0
SCALE_CAP = math.log(100.0)
BIAS_RANGE = 16.0
HIGHEST = lax.Precision.HIGHEST


def from_behind(block, axis, distance):
    devices = range(lax.axis_size(axis))
    route = [((i - distance) % len(devices), i) for i in devices]
    return lax.ppermute(block, axis, route)


def cut_along(value, dim, length):
    before, after = (value.shape[:dim], value.shape[dim + 1 :])
    return jnp.moveaxis(value.reshape(*before, length, -1, *after), dim, 0)


def summed_on_arrival(value, axis, dim):
    tiles = cut_along(value, dim, lax.axis_size(axis))
    arrived = lax.all_to_all(tiles, axis, split_axis=0, concat_axis=0, tiled=True)
    return arrived.sum(axis=0)


def summed_rows(value, axes, dim):
    far, near = axes
    tiles = cut_along(value, dim, lax.axis_size(far))
    nearer = summed_on_arrival(tiles, near, dim + 1)
    arrived = lax.all_to_all(nearer, far, split_axis=0, concat_axis=0, tiled=True)
    return arrived.sum(axis=0)


def rows_for(lines, length):
    spare = -lines.shape[0] % length
    if not spare:
        return lines
    return jnp.concatenate([lines, jnp.zeros((spare, *lines.shape[1:]), lines.dtype)])


def sent_to_all(value, axis):
    copies = jnp.broadcast_to(value, (lax.axis_size(axis), *value.shape))
    return lax.all_to_all(copies, axis, split_axis=0, concat_axis=0, tiled=True)


def joined_along(tiles, dim):
    tiles = jnp.moveaxis(tiles, 0, dim)
    dims = tiles.shape
    return tiles.reshape(*dims[:dim], dims[dim] * dims[dim + 1], *dims[dim + 2 :])


def gather_axes(value, axes, dim):
    far, near = axes
    tiles = sent_to_all(sent_to_all(value, far), near)
    return joined_along(tiles.swapaxes(0, 1).reshape(-1, *value.shape), dim)


def nested_sum(value, axes):
    own = summed_rows(rows_for(value, lax.axis_size(axes[0]) * lax.axis_size(axes[1])), axes, 0)
    whole = gather_axes(own, axes, 0)
    return whole[: len(value)].reshape(value.shape)


def packed_total(arrays, axis):
    ends = [0]
    for a in arrays:
        ends.append(ends[-1] + a.size)
    running = nested_sum(jnp.concatenate([a.ravel() for a in arrays]), axis)
    return tuple((running[b:e].reshape(a.shape) for a, b, e in zip(arrays, ends, ends[1:])))


def sum_at_owner(value, axis, dim):
    tiles = cut_along(value, dim, lax.axis_size(axis))
    arrived = lax.all_to_all(tiles, axis, split_axis=0, concat_axis=0, tiled=True)
    return arrived.astype(jnp.float32).sum(axis=0)


def of_everyone(value, axis):
    return sent_to_all(value, axis).sum(axis=0)


def together(arrays, axis):
    ends = [0]
    for a in arrays:
        ends.append(ends[-1] + a.size)
    running = of_everyone(jnp.concatenate([a.ravel() for a in arrays]), axis)
    return tuple((running[b:e].reshape(a.shape) for a, b, e in zip(arrays, ends, ends[1:])))


def coarse_product(form, left, right):
    return jnp.einsum(form, left, right, preferred_element_type=jnp.float32)


def fine_product(form, left, right):
    return jnp.einsum(form, left, right, precision=HIGHEST)


def to_windows(block, window):
    images, height, width, depth = block.shape
    tiles = block.reshape(images, height // window, window, width // window, window, depth)
    tiles = tiles.transpose(0, 1, 3, 2, 4, 5)
    return tiles.reshape(images, height // window * (width // window), window * window, depth)


def from_windows(tiles, images, height, width, window):
    depth = tiles.shape[-1]
    grid = tiles.reshape(images, height // window, width // window, window, window, depth)
    return grid.transpose(0, 1, 3, 2, 4, 5).reshape(images, height, width, depth)


def position_onehot(window):
    places = jnp.arange(window * window, dtype=jnp.int32)
    row_of = places // window
    col_of = places % window
    offset = (row_of[:, None] - row_of[None, :] + window - 1) * (2 * window - 1) + (
        col_of[:, None] - col_of[None, :] + window - 1
    )
    entries = jnp.arange((2 * window - 1) ** 2, dtype=jnp.int32)
    return (offset.reshape(-1)[:, None] == entries[None, :]).astype(jnp.float32)


def region_of(coords, extent, window):
    return (coords >= extent - window).astype(jnp.int32) + (coords >= extent - window // 2).astype(
        jnp.int32
    )


def region_mask(row_start, col_start, rows, cols, height, width, window):
    row_label = region_of(row_start + jnp.arange(rows, dtype=jnp.int32), height, window)
    col_label = region_of(col_start + jnp.arange(cols, dtype=jnp.int32), width, window)
    labels = row_label[:, None] * 3 + col_label[None, :]
    labels = labels.reshape(rows // window, window, cols // window, window).transpose(0, 2, 1, 3)
    labels = labels.reshape(-1, window * window)
    return jnp.where(labels[:, :, None] != labels[:, None, :], MASK_FILL, 0.0).astype(jnp.float32)


def grads_region(block, grad_block, row_start, col_start, height, width, window, params):
    w_qkv, w_proj, table_logits, logit_scale, gain = params
    images, rows, cols, depth = block.shape
    heads = logit_scale.shape[0]
    head_dim = depth // heads
    tiles = to_windows(block, window)
    grad_tiles = to_windows(grad_block, window)
    count = tiles.shape[1]
    length = window * window
    flat = tiles.reshape(-1, depth)
    qkv = jnp.dot(flat, w_qkv, preferred_element_type=jnp.float32).astype(jnp.bfloat16)
    qkv = qkv.reshape(images, count, length, 3, heads, head_dim)
    query = qkv[:, :, :, 0].astype(jnp.float32)
    keys = qkv[:, :, :, 1].astype(jnp.float32)
    values = qkv[:, :, :, 2]
    query_inv = lax.rsqrt(jnp.sum(query * query, -1, keepdims=True) + 1.0)
    key_inv = lax.rsqrt(jnp.sum(keys * keys, -1, keepdims=True) + 1.0)
    unit_query = query * query_inv
    unit_key = keys * key_inv
    scale = jnp.exp(jnp.minimum(logit_scale, SCALE_CAP))
    onehot = position_onehot(window)
    sigma = jax.nn.sigmoid(table_logits)
    rel_bias = jnp.dot(sigma * BIAS_RANGE, onehot.T, precision=HIGHEST).reshape(
        heads, length, length
    )
    mask = region_mask(row_start, col_start, rows, cols, height, width, window)
    cosine = fine_product("bnqhd,bnkhd->bnhqk", unit_query, unit_key)
    scores = scale[:, None, None] * cosine + rel_bias[None, None] + mask[None, :, None]
    top = jnp.max(scores, -1, keepdims=True)
    expo = jnp.exp(scores - top)
    probs = expo / jnp.sum(expo, -1, keepdims=True)
    probs_low = probs.astype(jnp.bfloat16)
    attended = (
        coarse_product("bnhqk,bnkhd->bnqhd", probs_low, values)
        .astype(jnp.bfloat16)
        .reshape(-1, depth)
    )
    proj = jnp.dot(attended, w_proj, preferred_element_type=jnp.float32)
    centre = proj - jnp.mean(proj, -1, keepdims=True)
    inv_std = lax.rsqrt(jnp.mean(centre * centre, -1, keepdims=True) + EPS_NORM)
    normed = centre * inv_std
    upstream = grad_tiles.reshape(-1, depth).astype(jnp.float32)
    d_gain = jnp.sum(upstream * normed, 0)
    scaled = upstream * gain
    d_proj = inv_std * (
        scaled
        - jnp.mean(scaled, -1, keepdims=True)
        - normed * jnp.mean(scaled * normed, -1, keepdims=True)
    )
    d_proj = d_proj.astype(jnp.bfloat16)
    d_wproj = jnp.dot(attended.T, d_proj, preferred_element_type=jnp.float32)
    d_att = jnp.dot(d_proj, w_proj.T, preferred_element_type=jnp.float32).astype(jnp.bfloat16)
    d_att = d_att.reshape(images, count, length, heads, head_dim)
    d_probs = coarse_product("bnqhd,bnkhd->bnhqk", d_att, values)
    d_values = coarse_product("bnhqk,bnqhd->bnkhd", probs_low, d_att)
    d_scores = probs * (d_probs - jnp.sum(d_probs * probs, -1, keepdims=True))
    d_bias = jnp.sum(d_scores, (0, 1)).reshape(heads, length * length)
    d_table = jnp.dot(d_bias, onehot, precision=HIGHEST) * (BIAS_RANGE * sigma * (1.0 - sigma))
    live = (logit_scale < SCALE_CAP).astype(jnp.float32)
    d_scale = jnp.sum(d_scores * cosine, (0, 1, 3, 4)) * scale * live
    d_cos = d_scores * scale[:, None, None]
    d_unit_q = fine_product("bnhqk,bnkhd->bnqhd", d_cos, unit_key)
    d_unit_k = fine_product("bnhqk,bnqhd->bnkhd", d_cos, unit_query)
    d_query = query_inv * (
        d_unit_q - unit_query * jnp.sum(unit_query * d_unit_q, -1, keepdims=True)
    )
    d_key = key_inv * (d_unit_k - unit_key * jnp.sum(unit_key * d_unit_k, -1, keepdims=True))
    d_qkv = jnp.stack([d_query, d_key, d_values], 3).astype(jnp.bfloat16).reshape(-1, 3 * depth)
    d_wqkv = jnp.dot(flat.T, d_qkv, preferred_element_type=jnp.float32)
    d_flat = jnp.dot(d_qkv, w_qkv.T, preferred_element_type=jnp.float32).astype(jnp.bfloat16)
    d_block = from_windows(d_flat.reshape(images, count, length, depth), images, rows, cols, window)
    return (d_block, (d_wqkv, d_wproj, d_table, d_scale, d_gain))


def shift_in(tokens, cotangent, shift):
    stacked = jnp.stack([tokens, cotangent])
    below = from_behind(stacked[:, :, :shift], HA, -1)
    tall = jnp.concatenate([stacked[:, :, shift:], below], 2)
    beside = from_behind(tall[:, :, :, :shift], WA, -1)
    moved = jnp.concatenate([tall[:, :, :, shift:], beside], 3)
    return (moved[0], moved[1])


def shift_out(grads, shift):
    rows = grads.shape[1]
    cols = grads.shape[2]
    right = from_behind(grads[:, :, cols - shift :], WA, 1)
    wide = jnp.concatenate([right, grads[:, :, : cols - shift]], 2)
    lower = from_behind(wide[:, rows - shift :], HA, 1)
    return jnp.concatenate([lower, wide[:, : rows - shift]], 1)


def shards(tokens, cotangent, w_qkv, w_proj, table_logits, logit_scale, gain):
    rows = tokens.shape[1]
    cols = tokens.shape[2]
    shift = WIN // 2
    height = rows * lax.axis_size(HA)
    width = cols * lax.axis_size(WA)
    row_base = lax.axis_index(HA) * rows
    col_base = lax.axis_index(WA) * cols
    params = (w_qkv, w_proj, table_logits, logit_scale, gain)
    moved, moved_grad = shift_in(tokens, cotangent, shift)
    d_moved, parts = grads_region(moved, moved_grad, row_base, col_base, height, width, WIN, params)
    back = shift_out(d_moved, shift)
    d_tokens = (cotangent.astype(jnp.float32) + back.astype(jnp.float32)).astype(jnp.bfloat16)
    d_wqkv, d_wproj, d_table, d_scale, d_gain = parts
    d_wqkv, d_wproj, d_table, d_scale, d_gain = packed_total(
        (d_wqkv, d_wproj, d_table, d_scale, d_gain), (("ha_0", "ha_1", "wa_0"), "wa_1")
    )
    half_qkv, half_proj = (
        sum_at_owner(d_wqkv.astype(jnp.bfloat16), "ba", 1),
        sum_at_owner(d_wproj.astype(jnp.bfloat16), "ba", 1),
    )
    d_table, d_scale, d_gain = together((d_table, d_scale, d_gain), "ba")
    return (d_tokens, half_qkv, half_proj, d_table, d_scale, d_gain)


def solution(mesh):
    finer = Mesh(
        mesh.devices.reshape(8, 2, 4, 2, mesh.shape["ba"]), ("ha_0", "ha_1", "wa_0", "wa_1", "ba")
    )
    in_specs = (P("ba", HA, WA, None), P("ba", HA, WA, None), P(), P(), P(), P(), P())
    out_specs = (P("ba", HA, WA, None), P(None, "ba"), P(None, "ba"), P(), P(), P())
    return jax.shard_map(
        shards, mesh=finer, in_specs=in_specs, out_specs=out_specs, check_vma=False
    )
```

profile of v0, /device:TPU:1, one launch (start us, length us, event | category | flops | bytes accessed | tf_op | source)
XLA Modules:
  0.0 295.5 jit_solution(2320317348752213545)
XLA Ops:
  0.7 1.0 pad_maximum_fusion.2
  1.7 3.2 %collective-permute-start = (bf16[2,1,4,32,384]{4,3,2,1,0:T(8,128)(2,1)S(1)}, bf16[2,1,4,32,384]{4,3,2,1,0:T(8,128)(2,1)S(1)}, u32[]{:S(2)}, u32[]{:S(2)}) collective-permute-start(bf16[2,1,4,32,384]{4,3,2,1,0:T(8,128)(2,1)S(1)} %pad_maximum_fusion.2), channel_id=1, source_target_pairs={{16,0},{32,16},{48,32},{64,48},{80,64},{96,80},{112,96},{128,112},... | collective-permute-start | bytes 589832 | tf_op jit(solution)/shard_map/ppermute | solution.py:24
  4.9 1.1 fusion.52
  6.3 0.8 compare_select_fusion
  7.3 2.0 fusion.2
  9.5 0.9 copy.150
  10.4 2.0 collective-permute-start.1
  12.7 1.4 collective-permute-done.1
  14.1 0.9 fusion.57
  17.2 2.7 reshape.479
  20.0 1.8 fusion.67
  22.5 5.2 %fusion.29 = f32[8,12,64,64]{2,3,1,0:T(8,128)S(1)} fusion(f32[8,64,12]{1,2,0:T(8,128)S(1)} %add_rsqrt_fusion.1, f32[8,64,12]{1,2,0:T(8,128)S(1)} %add_rsqrt_fusion, bf16[1,8,64,1,12,32]{2,1,5,4,3,0:T(8,128)(2,1)S(1)} %get-tuple-element.35, bf16[1,8,64,1,12,32]{2,1,5,4,3,0:T(8,128)(2,1)S(1)} %get-tuple-element.36), kind=kOutput, calls=%fused_computation.41 | convolution fusion | flops 151781376 | bytes 2408448 | tf_op jit(solution)/shard_map/bnqhd,bnkhd->bnhqk/dot_general | solution.py:107
  27.7 1.2 fusion.68
  30.0 1.1 copy-done.3
  31.6 1.3 reshape.481
  32.9 1.5 fusion.69
  34.7 0.9 copy.154
  35.6 2.3 copy.155
  37.9 1.2 fusion.42
  39.0 1.4 multiply_reduce_fusion.2
  40.6 1.4 multiply_convert_fusion
  43.4 1.3 reshape.482
  44.7 3.9 %multiply_reduce_fusion.1 = (f32[8,12,64]{2,1,0:T(8,128)S(1)}, f32[8,12,64,64]{2,3,1,0:T(8,128)S(1)}) fusion(f32[8,12,64,64]{2,3,1,0:T(8,128)} %copy-done.3, f32[8,12,64]{2,1,0:T(8,128)S(1)} %get-tuple-element.40, bf16[1,8,64,1,12,32]{2,1,5,4,3,0:T(8,128)(2,1)} %copy-done.20, bf16[8,64,12,32]{1,0,3,2:T(8,128)(2,1)} %reshape.482), kind=kOutput, calls=%fused_computation.7 | convolution fusion | flops 26339328 | bytes 3981312 | tf_op jit(solution)/shard_map/bnqhd,bnkhd->bnhqk/dot_general | solution.py:103
  48.9 2.2 multiply_reduce_fusion
  51.1 3.2 %fusion.22 = (f32[8,64,12]{1,2,0:T(8,128)S(1)}, f32[8,12,32,64]{3,2,1,0:T(8,128)S(1)}) fusion(f32[8,64,12]{1,2,0:T(8,128)S(1)} %add_rsqrt_fusion.1, bf16[1,8,64,1,12,32]{2,1,5,4,3,0:T(8,128)(2,1)S(1)} %get-tuple-element.36, f32[8,12,64,64]{2,3,1,0:T(8,128)S(1)} %get-tuple-element.34, f32[12]{0:T(128)S(1)} %minimum_exponential_fusion, ...), kind=kOutput, calls=%fused_computation.35 | convolution fusion | flops 152561664 | bytes 3219504 | tf_op jit(solution)/shard_map/bnhqk,bnkhd->bnqhd/dot_general | solution.py:107
  54.4 5.1 %fusion.18 = (f32[8,64,12]{1,2,0:T(8,128)S(1)}, f32[8,12,32,64]{3,2,1,0:T(8,128)S(1)}) fusion(f32[8,64,12]{1,2,0:T(8,128)S(1)} %add_rsqrt_fusion, bf16[1,8,64,1,12,32]{2,1,5,4,3,0:T(8,128)(2,1)S(1)} %get-tuple-element.35, f32[8,12,64,64]{2,3,1,0:T(8,128)S(1)} %get-tuple-element.34, f32[12]{0:T(128)S(1)} %minimum_exponential_fusion, ...), kind=kOutput, calls=%fused_computation.31 | convolution fusion | flops 152561664 | bytes 3219504 | tf_op jit(solution)/shard_map/bnhqk,bnqhd->bnkhd/dot_general | solution.py:107
  59.5 0.9 convolution_bitcast_fusion
  60.6 1.2 fusion.71
  61.8 0.8 fusion.21
  63.2 2.9 copy.163
  66.1 2.4 convert_element_type.211
  68.5 2.1 fusion.70
  70.7 1.3 reshape.484
  72.0 0.9 reshape.485
  72.9 2.0 copy.165
  74.8 1.1 reshape.486
  76.0 2.1 fusion.41
  78.3 14.6 %concatenate.37 = f32[593024]{0:T(1024)} concatenate(f32[442368]{0:T(1024)S(1)} %copy-done.5, f32[147456]{0:T(1024)S(1)} %copy-done.16, f32[2700]{0:T(1024)S(1)} %reshape.487, f32[12]{0:T(128)S(1)} %compare_select_fusion.1, f32[384]{0:T(512)S(1)} %get-tuple-element.32, f32[104]{0:T(128)S(1)} %broadcast_in_dim.18), dimensions={0} | concatenate | bytes 4744192 | tf_op jit(solution)/shard_map/concatenate | solution.py:50
  92.8 4.1 %reshape_reshape.15 = f32[64,2,4633]{2,1,0:T(2,128)S(1)} reshape(f32[593024]{0:T(1024)} %concatenate.37) | data formatting | bytes 4744192 | tf_op jit(solution)/shard_map/reshape;reshape | solution.py:29
  97.1 24.9 %all_to_all.44 = f32[2,64,4633]{2,1,0:T(8,128)S(1)} all-to-all(f32[2,64,4633]{2,1,0:T(8,128)S(1)} %copy.167), channel_id=1, replica_groups=mesh['ha_0'=8,'ha_1'=2,'wa_0'=4,'wa_1'=2,'ba'=2] {'wa_1'}, dimensions={0} | all-to-all | bytes 4744192 | tf_op jit(solution)/shard_map/all_to_all | solution.py:34
  122.0 1.3 reduce_sum.175
  123.2 2.1 all_to_all.29
  125.4 50.4 %all_to_all.45 = f32[64,1,4633]{2,1,0:T(1,128)S(1)} all-to-all(f32[64,1,4633]{2,1,0:T(1,128)S(1)} %all_to_all.29), channel_id=1, replica_groups=mesh['ha_0'=8,'ha_1'=2,'wa_0'=4,'wa_1'=2,'ba'=2] {'ha_0','ha_1','wa_0'}, dimensions={0} | all-to-all | bytes 2372096 | tf_op jit(solution)/shard_map/all_to_all | solution.py:42
  177.1 37.7 %all_to_all.46 = f32[64,1,4633]{2,1,0:T(1,128)S(1)} all-to-all(f32[64,1,4633]{2,1,0:T(1,128)S(1)} %broadcast_in_dim.19), channel_id=1, replica_groups=mesh['ha_0'=8,'ha_1'=2,'wa_0'=4,'wa_1'=2,'ba'=2] {'ha_0','ha_1','wa_0'}, dimensions={0} | all-to-all | bytes 2372096 | tf_op jit(solution)/shard_map/all_to_all | solution.py:55
  215.0 1.6 broadcast_in_dim.20
  216.6 3.8 %all-to-all-start.3 = ((f32[2,64,4633]{2,1,0:T(8,128)}), f32[2,64,4633]{2,1,0:T(8,128)S(1)}, u32[]{:S(2)}, u32[]{:S(2)}) async-start(f32[2,64,4633]{2,1,0:T(8,128)} %broadcast_in_dim.20), calls=%async_computation.3 | async-start | bytes 4849664 | tf_op jit(solution)/shard_map/all_to_all | solution.py:55
  220.4 2.1 convolution_convert_fusion.2
  223.3 1.4 collective-permute-start.2
  224.8 22.4 %all-to-all-done.3 = f32[2,64,4633]{2,1,0:T(8,128)S(1)} async-done(((f32[2,64,4633]{2,1,0:T(8,128)}), f32[2,64,4633]{2,1,0:T(8,128)S(1)}, u32[]{:S(2)}, u32[]{:S(2)}) %all-to-all-start.3) | async-done | bytes 2372128 | tf_op jit(solution)/shard_map/all_to_all | solution.py:55
  247.2 3.3 %copy.168 = f32[64,2,4633]{2,1,0:T(2,128)} copy(f32[64,2,4633]{2,0,1:T(8,128)S(1)} %bitcast.140) | data formatting | bytes 4744192 | tf_op jit(solution)/shard_map/transpose | solution.py:67
  250.5 3.7 %reshape_reshape.16 = f32[593024]{0:T(1024)S(1)} reshape(f32[64,2,4633]{2,1,0:T(2,128)} %copy.168) | data formatting | bytes 4744192 | tf_op jit(solution)/shard_map/reshape;reshape | solution.py:61
  254.8 3.7 %all-to-all-start.6 = ((f32[2,1,3096]{2,1,0:T(1,128)}), f32[2,1,3096]{2,1,0:T(1,128)S(1)}, u32[]{:S(2)}, u32[]{:S(2)}) async-start(f32[2,1,3096]{2,1,0:T(1,128)} %broadcast_in_dim.21), calls=%async_computation.6 | async-start | bytes 51200 | tf_op jit(solution)/shard_map/all_to_all | solution.py:55
  258.7 1.0 copy-done.6
  259.9 1.3 copy.171
  261.2 1.6 all-to-all-done.6
  262.8 4.1 %all-to-all-start.5 = ((bf16[2,384,192]{1,2,0:T(8,128)(2,1)}), bf16[2,384,192]{1,2,0:T(8,128)(2,1)}, u32[]{:S(2)}, u32[]{:S(2)}) async-start(bf16[2,384,192]{1,2,0:T(8,128)(2,1)} %copy.171), calls=%async_computation.5 | async-start | bytes 589824 | tf_op jit(solution)/shard_map/all_to_all | solution.py:86
  267.6 5.3 %collective-permute-start.3 = (bf16[1,4,32,384]{3,2,1,0:T(8,128)(2,1)}, bf16[1,4,32,384]{3,2,1,0:T(8,128)(2,1)}, u32[]{:S(2)}, u32[]{:S(2)}) collective-permute-start(bf16[1,4,32,384]{3,2,1,0:T(8,128)(2,1)} %pad_maximum_fusion.3), channel_id=1, source_target_pairs={{240,0},{0,16},{16,32},{32,48},{48,64},{64,80},{80,96},{96,112},{1... | collective-permute-start | bytes 294920 | tf_op jit(solution)/shard_map/ppermute | solution.py:24
  273.0 0.8 convert_element_type.215
  273.8 2.9 copy.169
  276.7 4.6 %all-to-all-start.4 = ((bf16[2,384,576]{1,2,0:T(8,128)(2,1)}), bf16[2,384,576]{1,2,0:T(8,128)(2,1)S(1)}, u32[]{:S(2)}, u32[]{:S(2)}) async-start(bf16[2,384,576]{1,2,0:T(8,128)(2,1)} %copy.169), calls=%async_computation.4 | async-start | bytes 1769472 | tf_op jit(solution)/shard_map/all_to_all | solution.py:86
  281.3 1.8 add_convert_fusion
  285.1 1.7 convert_reduce_fusion.1
  286.8 7.4 %all-to-all-done.4 = bf16[2,384,576]{1,2,0:T(8,128)(2,1)S(1)} async-done(((bf16[2,384,576]{1,2,0:T(8,128)(2,1)}), bf16[2,384,576]{1,2,0:T(8,128)(2,1)S(1)}, u32[]{:S(2)}, u32[]{:S(2)}) %all-to-all-start.4) | async-done | bytes 884768 | tf_op jit(solution)/shard_map/all_to_all | solution.py:86
  294.2 1.0 convert_reduce_fusion
  (114 shorter events, 14.2 us)
Async XLA Ops:
  0.6 15.2 %copy-start = (bf16[384,1152]{1,0:T(8,128)(2,1)S(1)}, bf16[384,1152]{1,0:T(8,128)(2,1)}, u32[]{:S(2)}) copy-start(bf16[384,1152]{1,0:T(8,128)(2,1)} %param.9) | copy-start | bytes 2654212
  0.6 6.6 %copy-start.27 = (f32[12,225]{1,0:T(8,128)S(1)}, f32[12,225]{1,0:T(8,128)}, u32[]{:S(2)}) copy-start(f32[12,225]{1,0:T(8,128)} %param.11) | copy-start | bytes 32404
  1.7 8.7 %collective-permute-start = (bf16[2,1,4,32,384]{4,3,2,1,0:T(8,128)(2,1)S(1)}, bf16[2,1,4,32,384]{4,3,2,1,0:T(8,128)(2,1)S(1)}, u32[]{:S(2)}, u32[]{:S(2)}) collective-permute-start(bf16[2,1,4,32,384]{4,3,2,1,0:T(8,128)(2,1)S(1)} %pad_maximum_fusion.2), channel_id=1, source_target_pairs={{16,0},{32,16},{48,32},{64,48},{80,64},{96,80},{112,96},{128,112},... | collective-permute-start | bytes 589832 | tf_op jit(solution)/shard_map/ppermute | solution.py:24
  6.0 4.3 %copy-start.28 = (f32[12]{0:T(128)S(1)}, f32[12]{0:T(128)}, u32[]{:S(2)}) copy-start(f32[12]{0:T(128)} %param.12) | copy-start | bytes 148
  10.4 3.7 %collective-permute-start.1 = (bf16[2,1,16,4,384]{4,3,2,1,0:T(4,128)(2,1)S(1)}, bf16[2,1,16,4,384]{4,3,2,1,0:T(4,128)(2,1)S(1)}, u32[]{:S(2)}, u32[]{:S(2)}) collective-permute-start(bf16[2,1,16,4,384]{4,3,2,1,0:T(4,128)(2,1)S(1)} %pad_maximum_fusion.4), channel_id=1, source_target_pairs={{2,0},{4,2},{6,4},{8,6},{10,8},{12,10},{14,12},{0,14},{3,1},{5,3},... | collective-permute-start | bytes 294920 | tf_op jit(solution)/shard_map/ppermute | solution.py:24
  15.0 0.7 copy-start.9
  21.7 7.7 %copy-start.20 = (bf16[1,8,64,1,12,32]{2,1,5,4,3,0:T(8,128)(2,1)}, bf16[1,8,64,1,12,32]{2,1,5,4,3,0:T(8,128)(2,1)S(1)}, u32[]{:S(2)}) copy-start(bf16[1,8,64,1,12,32]{2,1,5,4,3,0:T(8,128)(2,1)S(1)} %get-tuple-element.37) | copy-start | bytes 1179652
  22.5 5.2 %copy-start.17 = (f32[12,64,64]{1,2,0:T(8,128)S(1)}, f32[12,64,64]{1,2,0:T(8,128)}, u32[]{:S(2)}) copy-start(f32[12,64,64]{1,2,0:T(8,128)} %copy.150) | copy-start | bytes 589828
  22.5 5.2 %copy-start.19 = (f32[8,64,64]{1,2,0:T(8,128)S(1)}, f32[8,64,64]{1,2,0:T(8,128)}, u32[]{:S(2)}) copy-start(f32[8,64,64]{1,2,0:T(8,128)} %compare_select_fusion) | copy-start | bytes 393220
  27.7 1.7 copy-start.1
  29.4 1.7 copy-start.3
  32.9 1.7 copy-start.13
  34.6 3.2 %copy-start.26 = (f32[384]{0:T(512)S(1)}, f32[384]{0:T(512)}, u32[]{:S(2)}) copy-start(f32[384]{0:T(512)} %param.13) | copy-start | bytes 4612
  40.6 2.2 copy-start.18
  42.0 0.8 copy-start.10
  44.7 3.9 %copy-start.2 = (f32[8,12,64,64]{2,3,1,0:T(8,128)S(1)}, f32[8,12,64,64]{2,3,1,0:T(8,128)}, u32[]{:S(2)}) copy-start(f32[8,12,64,64]{2,3,1,0:T(8,128)} %copy-done.1) | copy-start | bytes 4718596
  44.7 4.3 %copy-start.4 = (f32[8,12,64,64]{2,3,1,0:T(8,128)S(1)}, f32[8,12,64,64]{2,3,1,0:T(8,128)}, u32[]{:S(2)}) copy-start(f32[8,12,64,64]{2,3,1,0:T(8,128)} %copy-done.3) | copy-start | bytes 4718596
  54.3 5.1 %copy-start.21 = (bf16[8,64,12,32]{1,0,3,2:T(8,128)(2,1)S(1)}, bf16[8,64,12,32]{1,0,3,2:T(8,128)(2,1)}, u32[]{:S(2)}) copy-start(bf16[8,64,12,32]{1,0,3,2:T(8,128)(2,1)} %reshape.482) | copy-start | bytes 1179652
  59.5 1.0 copy-start.11
  59.5 1.1 copy-start.12
  70.7 1.3 copy-start.15
  72.0 6.2 %copy-start.5 = (f32[442368]{0:T(1024)S(1)}, f32[442368]{0:T(1024)}, u32[]{:S(2)}) copy-start(f32[442368]{0:T(1024)} %reshape.484) | copy-start | bytes 5308420
  72.9 5.4 %copy-start.16 = (f32[147456]{0:T(1024)S(1)}, f32[147456]{0:T(1024)}, u32[]{:S(2)}) copy-start(f32[147456]{0:T(1024)} %reshape.485) | copy-start | bytes 1769476
  216.6 30.6 %all-to-all-start.3 = ((f32[2,64,4633]{2,1,0:T(8,128)}), f32[2,64,4633]{2,1,0:T(8,128)S(1)}, u32[]{:S(2)}, u32[]{:S(2)}) async-start(f32[2,64,4633]{2,1,0:T(8,128)} %broadcast_in_dim.20), calls=%async_computation.3 | async-start | bytes 4849664 | tf_op jit(solution)/shard_map/all_to_all | solution.py:55
  222.6 0.7 copy-start.7
  223.3 43.6 %collective-permute-start.2 = (bf16[1,16,4,384]{3,2,1,0:T(4,128)(2,1)S(1)}, bf16[1,16,4,384]{3,2,1,0:T(4,128)(2,1)S(1)}, u32[]{:S(2)}, u32[]{:S(2)}) collective-permute-start(bf16[1,16,4,384]{3,2,1,0:T(4,128)(2,1)S(1)} %slice.96), channel_id=1, source_target_pairs={{14,0},{0,2},{2,4},{4,6},{6,8},{8,10},{10,12},{12,14},{15,1},{1,3}... | collective-permute-start | bytes 147464 | tf_op jit(solution)/shard_map/ppermute | solution.py:24
  254.8 8.0 %all-to-all-start.6 = ((f32[2,1,3096]{2,1,0:T(1,128)}), f32[2,1,3096]{2,1,0:T(1,128)S(1)}, u32[]{:S(2)}, u32[]{:S(2)}) async-start(f32[2,1,3096]{2,1,0:T(1,128)} %broadcast_in_dim.21), calls=%async_computation.6 | async-start | bytes 51200 | tf_op jit(solution)/shard_map/all_to_all | solution.py:55
  258.7 1.0 copy-start.6
  259.7 7.3 %copy-start.8 = (bf16[1,2,8,4,8,384]{5,4,3,2,1,0:T(8,128)(2,1)S(1)}, bf16[1,2,8,4,8,384]{5,4,3,2,1,0:T(8,128)(2,1)}, u32[]{:S(2)}) copy-start(bf16[1,2,8,4,8,384]{5,4,3,2,1,0:T(8,128)(2,1)} %copy-done.7) | copy-start | bytes 1179652
  259.9 13.0 %slice-start = ((bf16[593024]{0:T(1024)(128)(2,1)}), bf16[442368]{0:T(1024)(128)(2,1)S(1)}, s32[]{:S(2)}) async-start(bf16[593024]{0:T(1024)(128)(2,1)} %copy-done.6), calls=%async_computation.7 | async-start | bytes 1769472 | tf_op jit(solution)/shard_map/slice | solution.py:81
  262.8 11.0 %copy-start.24 = (f32[2,1,3096]{2,1,0:T(1,128)}, f32[2,1,3096]{2,1,0:T(1,128)S(1)}, u32[]{:S(2)}) copy-start(f32[2,1,3096]{2,1,0:T(1,128)S(1)} %all-to-all-done.6) | copy-start | bytes 74308
  262.8 13.9 %all-to-all-start.5 = ((bf16[2,384,192]{1,2,0:T(8,128)(2,1)}), bf16[2,384,192]{1,2,0:T(8,128)(2,1)}, u32[]{:S(2)}, u32[]{:S(2)}) async-start(bf16[2,384,192]{1,2,0:T(8,128)(2,1)} %copy.171), calls=%async_computation.5 | async-start | bytes 589824 | tf_op jit(solution)/shard_map/all_to_all | solution.py:86
  266.9 6.8 %copy-start.22 = (bf16[1,16,4,384]{3,2,1,0:T(4,128)(2,1)}, bf16[1,16,4,384]{3,2,1,0:T(4,128)(2,1)S(1)}, u32[]{:S(2)}) copy-start(bf16[1,16,4,384]{3,2,1,0:T(4,128)(2,1)S(1)} %collective-permute-done.2) | copy-start | bytes 147460
  267.6 13.7 %collective-permute-start.3 = (bf16[1,4,32,384]{3,2,1,0:T(8,128)(2,1)}, bf16[1,4,32,384]{3,2,1,0:T(8,128)(2,1)}, u32[]{:S(2)}, u32[]{:S(2)}) collective-permute-start(bf16[1,4,32,384]{3,2,1,0:T(8,128)(2,1)} %pad_maximum_fusion.3), channel_id=1, source_target_pairs={{240,0},{0,16},{16,32},{32,48},{48,64},{64,80},{80,96},{96,112},{1... | collective-permute-start | bytes 294920 | tf_op jit(solution)/shard_map/ppermute | solution.py:24
  273.8 7.5 %copy-start.14 = (bf16[1,16,32,384]{3,2,1,0:T(8,128)(2,1)S(1)}, bf16[1,16,32,384]{3,2,1,0:T(8,128)(2,1)}, u32[]{:S(2)}) copy-start(bf16[1,16,32,384]{3,2,1,0:T(8,128)(2,1)} %param.8) | copy-start | bytes 1179652
  276.7 4.6 %copy-start.23 = (bf16[1,16,4,384]{3,2,1,0:T(4,128)(2,1)S(1)}, bf16[1,16,4,384]{3,2,1,0:T(4,128)(2,1)}, u32[]{:S(2)}) copy-start(bf16[1,16,4,384]{3,2,1,0:T(4,128)(2,1)} %copy-done.22) | copy-start | bytes 147460
  276.7 6.4 %copy-start.25 = (f32[2,1,3096]{2,1,0:T(1,128)S(1)}, f32[2,1,3096]{2,1,0:T(1,128)}, u32[]{:S(2)}) copy-start(f32[2,1,3096]{2,1,0:T(1,128)} %copy-done.24) | copy-start | bytes 74308
  276.7 17.5 %all-to-all-start.4 = ((bf16[2,384,576]{1,2,0:T(8,128)(2,1)}), bf16[2,384,576]{1,2,0:T(8,128)(2,1)S(1)}, u32[]{:S(2)}, u32[]{:S(2)}) async-start(bf16[2,384,576]{1,2,0:T(8,128)(2,1)} %copy.169), calls=%async_computation.4 | async-start | bytes 1769472 | tf_op jit(solution)/shard_map/all_to_all | solution.py:86
where the time goes:
time: 301 us; the launch traced here: 295 us
  blocking collectives  113 us (38%)
  local copies, waits for them, and re-layouts  67.1 us (22%)
  waiting for transfers between devices  32.8 us (11%)
  matrix products  31.2 us (10%)
  starting transfers between devices  28.3 us (9%)
  other arithmetic  21.5 us (7%)
    all_to_all x1, blocking collectives, summed_rows(): lax.all_to_all(nearer, far, split_axis=0, concat_axis=0, tiled=True)  50.4 us
    all_to_all x1, blocking collectives, sent_to_all(): return lax.all_to_all(copies, axis, split_axis=0, concat_axis=0, tiled=True)  37.7 us
    all_to_all x1, blocking collectives, summed_on_arrival(): lax.all_to_all(tiles, axis, split_axis=0, concat_axis=0, tiled=True)  24.9 us
    all_to_all x2, waiting for transfers between devices, sent_to_all(): return lax.all_to_all(copies, axis, split_axis=0, concat_axis=0, tiled=True)  24 us
    concatenate x1, local copies, waits for them, and re-layouts, rows_for(): jnp.concatenate([lines, jnp.zeros((spare, *lines.shape[1:]), lines.dtype)])  14.6 us
    dot_general x3, matrix products, fine_product(): return jnp.einsum(form, left, right, precision=HIGHEST)  13.5 us
    ppermute x4, starting transfers between devices, from_behind(): return lax.ppermute(block, axis, route)  12 us
    all_to_all x2, starting transfers between devices, sum_at_owner(): lax.all_to_all(tiles, axis, split_axis=0, concat_axis=0, tiled=True)  8.74 us
  transfers between devices with their start and end apart: 8, of which 4 were waited for; matrix products, arithmetic and copies ran while one was open for 9% of the time, Pallas kernels for 0%

commit v1 on v0

v1 whole, which is shorter than its diff:
```python
import functools
import math

import jax
import jax.numpy as jnp
from jax import lax
from jax.experimental import pallas as pl
from jax.experimental.pallas import tpu as pltpu
from jax.sharding import PartitionSpec as P

MESH = pl.DeviceIdType.MESH
F32 = jnp.float32
BF16 = jnp.bfloat16
HIGHEST = lax.Precision.HIGHEST

EPS_NORM = 1e-05
MASK_FILL = -100.0
OTHER_WINDOW = -1e30
SCALE_CAP = math.log(100.0)
BIAS_RANGE = 16.0

ROWS, COLS, C = 16, 32, 384
TOKENS = ROWS * COLS
HEADS = 12
GROUPS = 3
PER = 4
PAIRS = 4
TABLE = 225
CHUNKS = 3
BARRIER = 34

NT = (((1,), (1,)), ((), ()))
TN = (((0,), (0,)), ((), ()))
NN = (((1,), (0,)), ((), ()))


def dot(a, b, dims=NN):
    return lax.dot_general(a, b, dims, preferred_element_type=F32)


def fine(a, b, dims=NN):
    return lax.dot_general(a, b, dims, precision=HIGHEST, preferred_element_type=F32)


def iota(shape, dim):
    return lax.broadcasted_iota(jnp.int32, shape, dim)


def split(x):
    high = x.astype(BF16)
    low = (x - high.astype(F32)).astype(BF16)
    return jnp.concatenate([high, low], axis=1)


def offset_onehot():
    entry = iota((TABLE, 256), 0)
    row = lax.shift_right_logical(entry * 4370, 16)
    col = entry - 15 * row
    lane = (row - 7) * 16 + (col - 7)
    lane = jnp.where(lane < 0, lane + 256, lane)
    return (lane == iota((TABLE, 256), 1)).astype(F32)


def remote(src, dst, send, recv, device):
    return pltpu.make_async_remote_copy(
        src_ref=src, dst_ref=dst, send_sem=send, recv_sem=recv, device_id=device, device_id_type=MESH
    )


def kernel(
    tok, cot, wqkv, wproj, table, lscale, gain,
    dtok_o, f_s, total_o,
    pk_send, rows_recv, pk_recv, cr_recv,
    x_s, c_s, qkv_s, qinv_s, kinv_s, qrow_s, bias_s, mask_s, p_s, raw_s, att_s, datt_s, dproj_s, dqkv_s, dbias_s, dm_s,
    rows_send2, pk_send2, rows_recv2, pk_recv2, cr_recv2,
    keep_k, g_s, core_recv, s1_s, xy_recv, z_buf,
    sm_s, smc_recv, smx_buf, smz_buf, smf_buf,
    hsem_s, hsem_r, csem_s, csem_r, xsem_s, xsem_r, zsem_s, zsem_r, fsem_s, fsem_r,
):
    ha, wa, ba = lax.axis_index("ha"), lax.axis_index("wa"), lax.axis_index("ba")
    core = ha % 2
    deep = ha // 2
    other = ha + 1 - 2 * core
    up, down = (ha + 15) % 16, (ha + 1) % 16
    left, right = (wa + 7) % 8, (wa + 1) % 8
    mine = ba * 8 + wa
    row_mine = core * 8 + wa

    plane = []
    for d in range(1, 16):
        at = (mine + d) % 16
        plane.append((at // 8, at % 8))
    depth = [(deep + d) % 8 * 2 + core for d in range(1, 8)]
    level = []
    for d in range(1, 16):
        at = (row_mine + d) % 16
        level.append((deep * 2 + at // 8, at % 8))

    barrier = pltpu.get_barrier_semaphore()
    greeted = [(other, wa, ba)]
    greeted += [(ha, w, b) for b, w in plane]
    greeted += [(h, wa, ba) for h in depth]
    greeted += [(other, (wa + d) % 8, ba) for d in range(1, 8)]
    greeted += [(up, wa, ba), (down, wa, ba), (up, left, ba), (down, right, ba)]
    for device in greeted:
        pl.semaphore_signal(barrier, inc=1, device_id=device, device_id_type=MESH)

    sub8 = iota((8, C), 0) < 4

    for n, ref in enumerate((tok, cot)):
        for quad in range(4):
            x = ref[0, 4 * quad : 4 * quad + 4, 0:16, :].astype(F32).reshape(4, 2, 8, C)[:, 0]
            tiles = [jnp.where(sub8, x[2 * i], pltpu.roll(x[2 * i + 1], 4, 0)) for i in range(2)]
            pk_send[n, 16 * quad : 16 * quad + 16, :] = jnp.concatenate(tiles, 0).astype(BF16)

    onehot = offset_onehot()
    sigma = jax.nn.sigmoid(table[...])
    lanes = fine(sigma * BIAS_RANGE, onehot)
    for h in range(HEADS):
        line = jnp.broadcast_to(lanes[h : h + 1, :], (128, 256))
        bias_s[h] = pltpu.roll(line, 0, 1, stride=1, stride_axis=0)[:, :128]
    key, query = iota((128, 128), 0), iota((128, 128), 1)

    def bit(x, n):
        return lax.shift_right_logical(x, n) & 1

    apart = bit(key, 3) != bit(query, 3)
    low_rows = bit(key, 6) != bit(query, 6)
    low_cols = bit(key, 2) != bit(query, 2)
    second = bit(key, 3) == 1
    for pair in range(PAIRS):
        differ = jnp.zeros((128, 128), jnp.int32)
        if pair // 2 == 1:
            differ = jnp.where(low_rows, (ha == 15).astype(jnp.int32), differ)
        if pair % 2 == 1:
            differ = jnp.maximum(differ, jnp.where(low_cols & second, (wa == 7).astype(jnp.int32), 0))
        value = jnp.where(differ > 0, MASK_FILL, 0.0).astype(F32)
        mask_s[pair] = jnp.where(apart, OTHER_WINDOW, value)

    pl.semaphore_wait(barrier, BARRIER)
    halo = []
    for n, ref in enumerate((tok, cot)):
        halo.append(remote(ref.at[0, pl.ds(0, 4)], rows_recv.at[n], hsem_s.at[3 * n], hsem_r.at[3 * n], (up, wa, ba)))
        halo.append(remote(pk_send.at[n], pk_recv.at[n], hsem_s.at[3 * n + 1], hsem_r.at[3 * n + 1], (ha, left, ba)))
        halo.append(
            remote(pk_send.at[n, pl.ds(0, 16)], cr_recv.at[n], hsem_s.at[3 * n + 2], hsem_r.at[3 * n + 2], (up, left, ba))
        )
    for copy in halo:
        copy.start()
    for copy in halo:
        copy.wait()

    for n, (ref, out) in enumerate(((tok, x_s), (cot, c_s))):
        for quad in range(4):
            if quad < 3:
                rows = ref[0, 4 * quad + 4 : 4 * quad + 8]
                pack = pk_recv[n, 16 * quad + 16 : 16 * quad + 32, :]
            else:
                rows, pack = rows_recv[n], cr_recv[n]
            x = pltpu.roll(rows.astype(F32).reshape(16, 8, C), 4, 1).reshape(4, 4, 8, C)
            pack = pack.astype(F32).reshape(2, 8, C)
            for pair in range(2):
                parts = []
                for i in range(4):
                    for j in (2 * pair, 2 * pair + 1):
                        if j < 3:
                            after = x[i, j + 1]
                        else:
                            after = pack[i // 2] if i % 2 else pltpu.roll(pack[i // 2], 4, 0)
                        parts.append(jnp.where(sub8, x[i, j], after))
                at = (quad // 2 * 2 + pair) * 128 + quad % 2 * 64
                out[at : at + 64, :] = jnp.concatenate(parts, 0).astype(BF16)

    for part in range(3):
        for half in range(2):
            at = slice(256 * half, 256 * half + 256)
            y = dot(x_s[at, :], wqkv[:, C * part : C * part + C]).astype(BF16)
            for g in range(GROUPS):
                qkv_s[3 * part + g, at, :] = y[:, 128 * g : 128 * g + 128]

    head_lanes = [(lax.shift_right_logical(iota((1, 128), 1), 5) == h) for h in range(PER)]
    head_mask = [m.astype(F32).astype(BF16) for m in head_lanes]
    same = (lax.shift_right_logical(iota((256, 128), 0) & 127, 5) == lax.shift_right_logical(iota((256, 128), 1), 5))
    same = same.astype(F32).astype(BF16)
    pick = (lax.shift_right_logical(iota((8, 256), 1) & 127, 5) == iota((8, 256), 0)).astype(F32).astype(BF16)
    scales = jnp.exp(jnp.minimum(lscale[...], SCALE_CAP))

    def stacked(x):
        return jnp.concatenate([x * m for m in head_mask], axis=0)

    def across(x, h):
        return jnp.broadcast_to(x[:, 32 * h : 32 * h + 1], (128, 128))

    for g in range(GROUPS):
        scale_rows = jnp.concatenate(
            [jnp.broadcast_to(scales[:, PER * g + h : PER * g + h + 1], (1, 128)) for h in range(PER)], axis=0
        )

        def forward(pair, carry, g=g, scale_rows=scale_rows):
            at = pl.ds(pl.multiple_of(pair * 128, 128), 128)
            q, k, v = qkv_s[g, at, :], qkv_s[3 + g, at, :], qkv_s[6 + g, at, :]
            qf, kf = q.astype(F32), k.astype(F32)
            q2, k2 = split(qf * qf), split(kf * kf)
            qinv_s[g, at, :] = lax.rsqrt(dot(q2, same) + 1.0)
            kinv = lax.rsqrt(dot(k2, same) + 1.0)
            kinv_s[g, at, :] = kinv
            qrow = lax.rsqrt(dot(pick, q2, NT) + 1.0)[0:PER] * scale_rows
            qrow_s[g, pair, 0:PER, :] = qrow
            raw = dot(stacked(k), q, NT)
            low = []
            for h in range(PER):
                z = raw[128 * h : 128 * h + 128] * across(kinv, h) * qrow[h : h + 1]
                raw_s[g, pair, 128 * h : 128 * h + 128, :] = z
                z = z + bias_s[PER * g + h] + mask_s[pair]
                e = jnp.exp(z - jnp.max(z, axis=0, keepdims=True))
                p = e * (1.0 / jnp.sum(e, axis=0, keepdims=True))
                p_s[g, pair, 128 * h : 128 * h + 128, :] = p
                low.append(p.astype(BF16))
            att_s[g, at, :] = dot(jnp.concatenate(low, axis=0), stacked(v), TN).astype(BF16)
            return carry

        lax.fori_loop(0, PAIRS, forward, 0)

    dgain = jnp.zeros((1, C), F32)
    for pair in range(PAIRS):
        at = slice(128 * pair, 128 * pair + 128)
        att = jnp.concatenate([att_s[g, at, :] for g in range(GROUPS)], axis=1)
        proj = dot(att, wproj[...])
        centre = proj - jnp.mean(proj, -1, keepdims=True)
        inv_std = lax.rsqrt(jnp.mean(centre * centre, -1, keepdims=True) + EPS_NORM)
        normed = centre * inv_std
        upstream = c_s[at, :].astype(F32)
        dgain = dgain + jnp.sum(upstream * normed, 0, keepdims=True)
        scaled = upstream * gain[...].reshape(1, C)
        dproj = inv_std * (
            scaled - jnp.mean(scaled, -1, keepdims=True) - normed * jnp.mean(scaled * normed, -1, keepdims=True)
        )
        dproj = dproj.astype(BF16)
        dproj_s[at, :] = dproj
        datt = dot(dproj, wproj[...], NT).astype(BF16)
        for g in range(GROUPS):
            datt_s[g, at, :] = datt[:, 128 * g : 128 * g + 128]
    for g in range(GROUPS):
        sm_s[25 + g : 26 + g, :] = dgain[:, 128 * g : 128 * g + 128]
    sm_s[28:32, :] = jnp.zeros((4, 128), F32)

    att = [att_s[g] for g in range(GROUPS)]
    rows = [dot(dproj_s[...], a, TN).astype(BF16).reshape(2, 12, 16, 128) for a in att]
    for g in range(GROUPS):
        for half in range(2):
            g_s[0, 1, half, :, :, 128 * g : 128 * g + 128] = rows[g][half, 0:8]
            g_s[1, 1, half, 4:8, :, 128 * g : 128 * g + 128] = rows[g][half, 8:12]

    def core_copy(c):
        return remote(g_s.at[c, 1 - core], core_recv.at[c], csem_s.at[c], csem_r.at[c], (other, wa, ba))

    def plane_copies(c):
        return [
            remote(
                s1_s.at[c, b, w], xy_recv.at[c, d], xsem_s.at[c, d], xsem_r.at[c, d], (ha, w, b)
            )
            for d, (b, w) in enumerate(plane)
        ]

    def depth_copies(c):
        return [
            remote(z_buf.at[c, deep], z_buf.at[c, deep], zsem_s.at[c, d], zsem_r.at[c, d], (h, wa, ba))
            for d, h in enumerate(depth)
        ]

    def level_copies(c):
        return [
            remote(f_s.at[c, row_mine], f_s.at[c, row_mine], fsem_s.at[c, d], fsem_r.at[c, d], (h, w, ba))
            for d, (h, w) in enumerate(level)
        ]

    def wait_depth(c):
        for d in range(1, 8):
            at = (deep + 8 - d) % 8
            copy = remote(
                z_buf.at[c, deep], z_buf.at[c, at], zsem_s.at[c, d - 1], zsem_r.at[c, d - 1], (depth[d - 1], wa, ba)
            )
            copy.wait_send()
            copy.wait_recv()

    def wait_level(c):
        for d in range(1, 16):
            at = (row_mine + 16 - d) % 16
            h, w = level[d - 1]
            copy = remote(f_s.at[c, row_mine], f_s.at[c, at], fsem_s.at[c, d - 1], fsem_r.at[c, d - 1], (h, w, ba))
            copy.wait_send()
            copy.wait_recv()

    def start_all(copies):
        for copy in copies:
            copy.start()

    def to_plane(c):
        core_copy(c).wait()
        for b in range(2):
            s1_s[c, b] = (g_s[c, core, b].astype(F32) + core_recv[c, b].astype(F32)).astype(BF16)
        start_all(plane_copies(c))

    def to_depth(c):
        for copy in plane_copies(c):
            copy.wait()
        total = s1_s[c, ba, wa].astype(F32)
        for d in range(15):
            total = total + xy_recv[c, d].astype(F32)
        z_buf[c, deep] = total.astype(BF16)
        start_all(depth_copies(c))

    def to_level(c):
        wait_depth(c)
        total = z_buf[c, 0].astype(F32)
        for d in range(1, 8):
            total = total + z_buf[c, d].astype(F32)
        f_s[c, row_mine] = total.astype(BF16)
        start_all(level_copies(c))

    for g in range(GROUPS):

        def backward(pair, dscale, g=g):
            at = pl.ds(pl.multiple_of(pair * 128, 128), 128)
            q, k, v = qkv_s[g, at, :], qkv_s[3 + g, at, :], qkv_s[6 + g, at, :]
            datt = datt_s[g, at, :]
            qinv, kinv = qinv_s[g, at, :], kinv_s[g, at, :]
            raw = dot(stacked(v), datt, NT)
            low, grads, sums = [], [], []
            for h in range(PER):
                p = p_s[g, pair, 128 * h : 128 * h + 128, :]
                dp = raw[128 * h : 128 * h + 128]
                ds = p * (dp - jnp.sum(dp * p, axis=0, keepdims=True))
                dbias_s[PER * g + h] = jnp.where(pair == 0, 0.0, dbias_s[PER * g + h]) + ds
                sums.append(jnp.sum(ds * raw_s[g, pair, 128 * h : 128 * h + 128, :], axis=0, keepdims=True))
                grads.append((ds * across(kinv, h) * qrow_s[g, pair, h : h + 1, :]).astype(BF16))
                low.append(p.astype(BF16))
            dv = dot(jnp.concatenate(low, axis=1), stacked(datt))
            a = dot(jnp.concatenate(grads, axis=0), stacked(k), TN)
            b = dot(jnp.concatenate(grads, axis=1), stacked(q))
            qf, kf = q.astype(F32), k.astype(F32)
            uq, uk = qf * qinv, kf * kinv
            dq = a - uq * dot(split(uq * a), same)
            dk = b - uk * dot(split(uk * b), same)
            dqkv_s[g, at, 0:128] = dq.astype(BF16)
            dqkv_s[g, at, 128:256] = dk.astype(BF16)
            dqkv_s[g, at, 256:384] = dv.astype(BF16)
            return dscale + jnp.concatenate(sums, axis=0)

        dscale = lax.fori_loop(0, PAIRS, backward, jnp.zeros((PER, 128), F32))
        here = iota((PER, 128), 0) + PER * g == iota((PER, 128), 1)
        spread = jnp.where(here, jnp.sum(dscale, axis=1, keepdims=True), 0.0)
        spread = jnp.sum(spread, axis=0, keepdims=True)
        scale_row = spread if g == 0 else scale_row + spread
        for part in range(3):
            dw = dot(dqkv_s[g, :, 128 * part : 128 * part + 128], x_s[...], TN).astype(BF16).reshape(8, 16, C)
            if part == 0:
                g_s[g, 0, 0] = dw
            elif part == 2:
                g_s[g, 0, 1] = dw
            elif g == 0:
                keep_k[...] = dw
            elif g == 1:
                g_s[1, 1, 0, 0:4] = dw[0:4]
                g_s[1, 1, 1, 0:4] = dw[4:8]
            else:
                g_s[2, 1, 0] = keep_k[...]
                g_s[2, 1, 1] = dw
        core_copy(g).start()
        if g > 0:
            to_plane(g - 1)

    sm_s[24:25, :] = scale_row

    lane8, sub256 = iota((8, 128), 1), iota((8, 256), 0)
    for h in range(HEADS):
        ahead = dbias_s[h, 0:8, :]
        behind = jnp.zeros((8, 128), F32)
        for n in range(1, 16):
            turned = pltpu.roll(dbias_s[h, 8 * n : 8 * n + 8, :], 128 - 8 * n, 1)
            inside = lane8 < 128 - 8 * n
            ahead = ahead + jnp.where(inside, turned, 0.0)
            behind = behind + jnp.where(inside, 0.0, turned)
        both = jnp.concatenate([ahead, behind], axis=1)
        for n in range(3):
            both = jnp.where(bit(sub256, n) == 1, pltpu.roll(both, 256 - 2**n, 1), both)
        both = jnp.sum(both, axis=0, keepdims=True)
        sm_s[h : h + 1, :] = both[:, 0:128]
        sm_s[12 + h : 13 + h, :] = both[:, 128:256]
    small_core = remote(
        sm_s.at[pl.ds(pl.multiple_of(16 * (1 - core), 16), 16)], smc_recv, csem_s.at[3], csem_r.at[3], (other, wa, ba)
    )
    small_core.start()

    to_plane(2)

    for pair in range(PAIRS):
        at = slice(128 * pair, 128 * pair + 128)
        total = jnp.zeros((128, C), F32)
        for g in range(GROUPS):
            w = jnp.concatenate([wqkv[:, C * n + 128 * g : C * n + 128 * g + 128] for n in range(3)], axis=1)
            total = total + dot(dqkv_s[g, at, :], w, NT)
        dm_s[at, :] = total.astype(BF16)

    def image_rows(quad):
        parts = []
        for i in range(4):
            for pair in range(2):
                at = (quad // 2 * 2 + pair) * 128 + quad % 2 * 64 + 16 * i
                parts.append(dm_s[at : at + 16, :])
        return jnp.concatenate(parts, axis=0).reshape(4, 32, C)

    for quad in range(4):
        x = image_rows(quad)
        if quad == 3:
            rows_send2[...] = x
        x = x.astype(F32).reshape(4, 4, 8, C)
        tiles = [jnp.where(sub8, pltpu.roll(x[2 * i, 3], 4, 0), x[2 * i + 1, 3]) for i in range(2)]
        pk_send2[16 * quad : 16 * quad + 16, :] = jnp.concatenate(tiles, 0).astype(BF16)
    halo = [
        remote(rows_send2, rows_recv2, hsem_s.at[6], hsem_r.at[6], (down, wa, ba)),
        remote(pk_send2, pk_recv2, hsem_s.at[7], hsem_r.at[7], (ha, right, ba)),
        remote(pk_send2.at[pl.ds(48, 16)], cr_recv2, hsem_s.at[8], hsem_r.at[8], (down, right, ba)),
    ]
    start_all(halo)

    small_core.wait()
    mine16 = sm_s[pl.ds(pl.multiple_of(16 * core, 16), 16), :]
    smx_buf[mine] = mine16 + smc_recv[...]
    small_plane = [
        remote(smx_buf.at[mine], smx_buf.at[mine], xsem_s.at[3, d], xsem_r.at[3, d], (ha, w, b))
        for d, (b, w) in enumerate(plane)
    ]
    start_all(small_plane)

    for c in range(CHUNKS):
        to_depth(c)

    for d in range(1, 16):
        at = (mine + 16 - d) % 16
        b, w = plane[d - 1]
        copy = remote(smx_buf.at[mine], smx_buf.at[at], xsem_s.at[3, d - 1], xsem_r.at[3, d - 1], (ha, w, b))
        copy.wait_send()
        copy.wait_recv()
    total = smx_buf[0]
    for d in range(1, 16):
        total = total + smx_buf[d]
    smz_buf[deep] = total
    small_depth = [
        remote(smz_buf.at[deep], smz_buf.at[deep], zsem_s.at[3, d], zsem_r.at[3, d], (h, wa, ba))
        for d, h in enumerate(depth)
    ]
    start_all(small_depth)

    for copy in halo:
        copy.wait()
    for quad in range(4):
        if quad == 0:
            rows, pack = rows_recv2[...], cr_recv2[...]
        else:
            rows, pack = image_rows(quad - 1), pk_recv2[16 * quad - 16 : 16 * quad, :]
        x = pltpu.roll(rows.astype(F32).reshape(16, 8, C), 4, 1).reshape(4, 4, 8, C)
        pack = pack.astype(F32).reshape(2, 8, C)
        for i in range(4):
            parts = []
            for j in range(4):
                if j > 0:
                    before = x[i, j - 1]
                else:
                    before = pltpu.roll(pack[i // 2], 4, 0) if i % 2 else pack[i // 2]
                parts.append(jnp.where(sub8, before, x[i, j]))
            back = jnp.concatenate(parts, 0)
            row = 4 * quad + i
            dtok_o[0, row] = (cot[0, row].astype(F32) + back).astype(BF16)

    for c in range(CHUNKS):
        to_level(c)

    for d in range(1, 8):
        at = (deep + 8 - d) % 8
        copy = remote(
            smz_buf.at[deep], smz_buf.at[at], zsem_s.at[3, d - 1], zsem_r.at[3, d - 1], (depth[d - 1], wa, ba)
        )
        copy.wait_send()
        copy.wait_recv()
    total = smz_buf[0]
    for d in range(1, 8):
        total = total + smz_buf[d]
    smf_buf[core] = total
    small_last = remote(smf_buf.at[core], smf_buf.at[core], csem_s.at[4], csem_r.at[4], (other, wa, ba))
    small_last.start()

    for c in range(CHUNKS):
        wait_level(c)

    copy = remote(smf_buf.at[core], smf_buf.at[1 - core], csem_s.at[4], csem_r.at[4], (other, wa, ba))
    copy.wait_send()
    copy.wait_recv()
    total_o[0:16, :] = smf_buf[0]
    total_o[16:32, :] = smf_buf[1]


def finish(pieces, total, moved, table, lscale, dtok_o, dwqkv_o, dwproj_o, dtable_o, dscale_o, dgain_o):
    ba = lax.axis_index("ba")
    dtok_o[...] = moved[...]

    def rows(base, count):
        return pl.ds(pl.multiple_of(base, 64), count)

    def join(c, core, first, count):
        return pieces[c, 8 * core + first : 8 * core + first + count].reshape(16 * count, C).astype(F32)

    for c in range(CHUNKS):
        dwqkv_o[rows(128 * c + 192 * ba, 128), :] = join(c, 0, 0, 8)
    dwproj_o[0:128, :] = join(0, 1, 0, 8)
    dwqkv_o[rows(512 - 512 * ba, 64), :] = join(1, 1, 0, 4)
    dwproj_o[128:192, :] = join(1, 1, 4, 4)
    dwqkv_o[rows(384 - 320 * ba, 128), :] = join(2, 1, 0, 8)

    by_lane = jnp.concatenate([total[0:12], total[12:24]], axis=1)
    sigma = jax.nn.sigmoid(table[...])
    dtable_o[...] = fine(by_lane, offset_onehot(), NT) * (BIAS_RANGE * sigma * (1.0 - sigma))
    live = (lscale[...] < SCALE_CAP).astype(F32)
    dscale_o[...] = total[24:25, 0:HEADS] * live
    for g in range(GROUPS):
        dgain_o[pl.ds(128 * g, 128)] = total[25 + g]


def step(tokens, cotangent, w_qkv, w_proj, table_logits, logit_scale, gain):
    vmem = pl.BlockSpec(memory_space=pltpu.VMEM)
    middle = [
        jax.ShapeDtypeStruct((1, ROWS, COLS, C), BF16),
        jax.ShapeDtypeStruct((CHUNKS, 16, 16, C), BF16),
        jax.ShapeDtypeStruct((32, 128), F32),
    ]
    outs = [
        jax.ShapeDtypeStruct((1, ROWS, COLS, C), BF16),
        jax.ShapeDtypeStruct((576, C), F32),
        jax.ShapeDtypeStruct((192, C), F32),
        jax.ShapeDtypeStruct((HEADS, TABLE), F32),
        jax.ShapeDtypeStruct((1, HEADS), F32),
        jax.ShapeDtypeStruct((C,), F32),
    ]
    scratch = [
        pltpu.VMEM((2, 64, C), BF16),
        pltpu.VMEM((2, 4, COLS, C), BF16),
        pltpu.VMEM((2, 64, C), BF16),
        pltpu.VMEM((2, 16, C), BF16),
        pltpu.VMEM((TOKENS, C), BF16),
        pltpu.VMEM((TOKENS, C), BF16),
        pltpu.VMEM((9, TOKENS, 128), BF16),
        pltpu.VMEM((GROUPS, TOKENS, 128), F32),
        pltpu.VMEM((GROUPS, TOKENS, 128), F32),
        pltpu.VMEM((GROUPS, PAIRS, 8, 128), F32),
        pltpu.VMEM((HEADS, 128, 128), F32),
        pltpu.VMEM((PAIRS, 128, 128), F32),
        pltpu.VMEM((GROUPS, PAIRS, TOKENS, 128), F32),
        pltpu.VMEM((GROUPS, PAIRS, TOKENS, 128), F32),
        pltpu.VMEM((GROUPS, TOKENS, 128), BF16),
        pltpu.VMEM((GROUPS, TOKENS, 128), BF16),
        pltpu.VMEM((TOKENS, C), BF16),
        pltpu.VMEM((GROUPS, TOKENS, C), BF16),
        pltpu.VMEM((HEADS, 128, 128), F32),
        pltpu.VMEM((TOKENS, C), BF16),
        pltpu.VMEM((4, COLS, C), BF16),
        pltpu.VMEM((64, C), BF16),
        pltpu.VMEM((4, COLS, C), BF16),
        pltpu.VMEM((64, C), BF16),
        pltpu.VMEM((16, C), BF16),
        pltpu.VMEM((8, 16, C), BF16),
        pltpu.VMEM((CHUNKS, 2, 2, 8, 16, C), BF16),
        pltpu.VMEM((CHUNKS, 2, 8, 16, C), BF16),
        pltpu.VMEM((CHUNKS, 2, 8, 16, C), BF16),
        pltpu.VMEM((CHUNKS, 15, 16, C), BF16),
        pltpu.VMEM((CHUNKS, 8, 16, C), BF16),
        pltpu.VMEM((32, 128), F32),
        pltpu.VMEM((16, 128), F32),
        pltpu.VMEM((16, 16, 128), F32),
        pltpu.VMEM((8, 16, 128), F32),
        pltpu.VMEM((2, 16, 128), F32),
        pltpu.SemaphoreType.DMA((9,)),
        pltpu.SemaphoreType.DMA((9,)),
        pltpu.SemaphoreType.DMA((5,)),
        pltpu.SemaphoreType.DMA((5,)),
        pltpu.SemaphoreType.DMA((4, 15)),
        pltpu.SemaphoreType.DMA((4, 15)),
        pltpu.SemaphoreType.DMA((4, 7)),
        pltpu.SemaphoreType.DMA((4, 7)),
        pltpu.SemaphoreType.DMA((3, 15)),
        pltpu.SemaphoreType.DMA((3, 15)),
    ]
    lscale = logit_scale.reshape(1, HEADS)
    moved, pieces, total = pl.pallas_call(
        kernel,
        name="window_backward",
        out_shape=middle,
        in_specs=[vmem] * 7,
        out_specs=[vmem] * 3,
        scratch_shapes=scratch,
        compiler_params=pltpu.CompilerParams(collective_id=0, has_side_effects=True),
    )(tokens, cotangent, w_qkv, w_proj, table_logits, lscale, gain)
    d_tokens, d_wqkv, d_wproj, d_table, d_scale, d_gain = pl.pallas_call(
        finish, name="finish", out_shape=outs, in_specs=[vmem] * 5, out_specs=[vmem] * 6
    )(pieces, total, moved, table_logits, lscale)
    return d_tokens, d_wqkv.T, d_wproj.T, d_table, d_scale.reshape(HEADS), d_gain


def solution(mesh):
    image = P("ba", "ha", "wa", None)
    return jax.shard_map(
        step,
        mesh=mesh,
        in_specs=(image, image, P(), P(), P(), P(), P()),
        out_specs=(image, P(None, "ba"), P(None, "ba"), P(), P(), P()),
        check_vma=False,
    )
```

time: 301 us -> 64.2 us (0.21); the launches traced: 295 us -> 64.1 us
  blocking collectives: 113 us -> 0 us
  local copies, waits for them, and re-layouts: 67.1 us -> 0 us
  Pallas kernels: 0 us -> 63.4 us
  waiting for transfers between devices: 32.8 us -> 0 us
  matrix products: 31.2 us -> 0 us
  starting transfers between devices: 28.3 us -> 0 us
  other arithmetic: 21.5 us -> 0 us
    all_to_all x3 -> x0, blocking collectives: 113 us -> none  [the longest x1 50.4 us: summed_rows(): lax.all_to_all(nearer, far, split_axis=0, concat_axis=0, tiled=True)]
    pallas_call x0 -> x2, Pallas kernels: none -> 63.4 us  [the longest x1 60.8 us: step(): pl.pallas_call(kernel, name='window_backward', out_shape=middle, in_specs...]
    all_to_all x4 -> x0, waiting for transfers between devices: 31.4 us -> none  [the longest x2 24 us: sent_to_all(): return lax.all_to_all(copies, axis, split_axis=0, concat_axis=0, tiled=True)]
    dot_general x14 -> x0, matrix products: 31.2 us -> none  [the longest x3 13.5 us: fine_product(): return jnp.einsum(form, left, right, precision=HIGHEST)]
    all_to_all x4 -> x0, starting transfers between devices: 16.3 us -> none  [the longest x2 8.74 us: sum_at_owner(): lax.all_to_all(tiles, axis, split_axis=0, concat_axis=0, tiled=True)]
    concatenate x1 -> x0, local copies, waits for them, and re-layouts: 14.6 us -> none  [rows_for(): jnp.concatenate([lines, jnp.zeros((spare, *lines.shape[1:]), lines.dtype)])]
    ppermute x4 -> x0, starting transfers between devices: 12 us -> none  [from_behind(): return lax.ppermute(block, axis, route)]
    convert_element_type x9 -> x0, local copies, waits for them, and re-layouts: 10.9 us -> none  [the longest x2 5.34 us: grads_region(): jnp.stack([d_query, d_key, d_values], 3).astype(jnp.bfloat16)]
  transfers between devices with their start and end apart: 8 -> 0, of which waited for: 4 -> 0; matrix products, arithmetic and copies ran while one was open for 9% -> 0% of each run, Pallas kernels for 0% -> 0%
where the time goes in v1:
time: 64.2 us; the launch traced here: 64.1 us
  Pallas kernels  63.4 us (99%)
    pallas_call x1, Pallas kernels, step(): pl.pallas_call(kernel, name='window_backward', out_shape=middle, in_specs...  60.8 us
    pallas_call x1, Pallas kernels, step(): pl.pallas_call(finish, name='finish', out_shape=outs, in_specs=[vmem] * 5...  2.63 us

profile of v1, /device:TPU:1, one launch (start us, length us, event | category | flops | bytes accessed | tf_op | source)
XLA Modules:
  0.0 64.1 jit_solution(10004729801686075808)
XLA Ops:
  0.6 60.8 %window_backward.1 = (bf16[1,16,32,384]{3,2,1,0:T(8,128)(2,1)}, bf16[3,16,16,384]{3,2,1,0:T(8,128)(2,1)}, f32[32,128]{1,0:T(8,128)}) custom-call(bf16[1,16,32,384]{3,2,1,0:T(8,128)(2,1)} %tok.1, bf16[1,16,32,384]{3,2,1,0:T(8,128)(2,1)} %cot.1, bf16[384,1152]{1,0:T(8,128)(2,1)} %wqkv.1, bf16[384,384]{1,0:T(8,128)(2,1)} %wproj.1, f32[12,225]{1,0:T(8,128)} %table.3, ...), custom_call_target="tpu_custom_call" | custom-call | tf_op jit(solution)/shard_map/window_backward/pallas_call | solution.py:593
  61.4 2.6 %finish.1 = (bf16[1,16,32,384]{3,2,1,0:T(8,128)(2,1)}, f32[576,384]{1,0:T(8,128)}, f32[192,384]{1,0:T(8,128)}, f32[12,225]{1,0:T(8,128)}, f32[1,12]{1,0:T(1,128)}, /*index=5*/f32[384]{0:T(512)}) custom-call(bf16[3,16,16,384]{3,2,1,0:T(8,128)(2,1)} %get-tuple-element.15.pieces, f32[32,128]{1,0:T(8,128)} %get-tuple-element.16.total, ...), custom_call_target="tpu_custom_call" | custom-call | tf_op jit(solution)/shard_map/finish/pallas_call | solution.py:602

commit v2 on v1

--- a/solution.py
+++ b/solution.py
@@ -68,15 +68,25 @@
 
 
 def kernel(
-    tok, cot, wqkv, wproj, table, lscale, gain,
+    tok_h, cot_h, wqkv_h, wproj_h, table_h, lscale, gain,
     dtok_o, f_s, total_o,
+    tok, cot, wqkv, wproj, table,
     pk_send, rows_recv, pk_recv, cr_recv,
     x_s, c_s, qkv_s, qinv_s, kinv_s, qrow_s, bias_s, mask_s, p_s, raw_s, att_s, datt_s, dproj_s, dqkv_s, dbias_s, dm_s,
     rows_send2, pk_send2, rows_recv2, pk_recv2, cr_recv2,
     keep_k, g_s, core_recv, s1_s, xy_recv, z_buf,
     sm_s, smc_recv, smx_buf, smz_buf, smf_buf,
-    hsem_s, hsem_r, csem_s, csem_r, xsem_s, xsem_r, zsem_s, zsem_r, fsem_s, fsem_r,
+    lsem, hsem_s, hsem_r, csem_s, csem_r, xsem_s, xsem_r, zsem_s, zsem_r, fsem_s, fsem_r,
 ):
+    loads = [
+        pltpu.make_async_copy(src, dst, lsem.at[n])
+        for n, (src, dst) in enumerate(
+            ((tok_h, tok), (cot_h, cot), (table_h, table), (wqkv_h, wqkv), (wproj_h, wproj))
+        )
+    ]
+    for load in loads:
+        load.start()
+
     ha, wa, ba = lax.axis_index("ha"), lax.axis_index("wa"), lax.axis_index("ba")
     core = ha % 2
     deep = ha // 2
@@ -107,12 +117,17 @@
 
     sub8 = iota((8, C), 0) < 4
 
+
+    loads[0].wait()
+    loads[1].wait()
     for n, ref in enumerate((tok, cot)):
         for quad in range(4):
             x = ref[0, 4 * quad : 4 * quad + 4, 0:16, :].astype(F32).reshape(4, 2, 8, C)[:, 0]
             tiles = [jnp.where(sub8, x[2 * i], pltpu.roll(x[2 * i + 1], 4, 0)) for i in range(2)]
             pk_send[n, 16 * quad : 16 * quad + 16, :] = jnp.concatenate(tiles, 0).astype(BF16)
 
+
+    loads[2].wait()
     onehot = offset_onehot()
     sigma = jax.nn.sigmoid(table[...])
     lanes = fine(sigma * BIAS_RANGE, onehot)
@@ -137,46 +152,54 @@
         value = jnp.where(differ > 0, MASK_FILL, 0.0).astype(F32)
         mask_s[pair] = jnp.where(apart, OTHER_WINDOW, value)
 
+
     pl.semaphore_wait(barrier, BARRIER)
-    halo = []
     for n, ref in enumerate((tok, cot)):
-        halo.append(remote(ref.at[0, pl.ds(0, 4)], rows_recv.at[n], hsem_s.at[3 * n], hsem_r.at[3 * n], (up, wa, ba)))
-        halo.append(remote(pk_send.at[n], pk_recv.at[n], hsem_s.at[3 * n + 1], hsem_r.at[3 * n + 1], (ha, left, ba)))
-        halo.append(
-            remote(pk_send.at[n, pl.ds(0, 16)], cr_recv.at[n], hsem_s.at[3 * n + 2], hsem_r.at[3 * n + 2], (up, left, ba))
-        )
-    for copy in halo:
-        copy.start()
-    for copy in halo:
-        copy.wait()
-
-    for n, (ref, out) in enumerate(((tok, x_s), (cot, c_s))):
-        for quad in range(4):
+        remote(ref.at[0, pl.ds(0, 4)], rows_recv.at[n], hsem_s.at[0], hsem_r.at[0], (up, wa, ba)).start()
+        remote(pk_send.at[n], pk_recv.at[n], hsem_s.at[1], hsem_r.at[1], (ha, left, ba)).start()
+        remote(pk_send.at[n, pl.ds(0, 16)], cr_recv.at[n], hsem_s.at[2], hsem_r.at[2], (up, left, ba)).start()
+
+    def shifted(quad, pair):
+        for n, (ref, out) in enumerate(((tok, x_s), (cot, c_s))):
             if quad < 3:
                 rows = ref[0, 4 * quad + 4 : 4 * quad + 8]
-                pack = pk_recv[n, 16 * quad + 16 : 16 * quad + 32, :]
             else:
-                rows, pack = rows_recv[n], cr_recv[n]
+                rows = rows_recv[n]
             x = pltpu.roll(rows.astype(F32).reshape(16, 8, C), 4, 1).reshape(4, 4, 8, C)
-            pack = pack.astype(F32).reshape(2, 8, C)
-            for pair in range(2):
-                parts = []
-                for i in range(4):
-                    for j in (2 * pair, 2 * pair + 1):
-                        if j < 3:
-                            after = x[i, j + 1]
-                        else:
-                            after = pack[i // 2] if i % 2 else pltpu.roll(pack[i // 2], 4, 0)
-                        parts.append(jnp.where(sub8, x[i, j], after))
-                at = (quad // 2 * 2 + pair) * 128 + quad % 2 * 64
-                out[at : at + 64, :] = jnp.concatenate(parts, 0).astype(BF16)
-
-    for part in range(3):
-        for half in range(2):
-            at = slice(256 * half, 256 * half + 256)
-            y = dot(x_s[at, :], wqkv[:, C * part : C * part + C]).astype(BF16)
+            if pair == 1:
+                pack = pk_recv[n, 16 * quad + 16 : 16 * quad + 32, :] if quad < 3 else cr_recv[n]
+                pack = pack.astype(F32).reshape(2, 8, C)
+            parts = []
+            for i in range(4):
+                for j in (2 * pair, 2 * pair + 1):
+                    if j < 3:
+                        after = x[i, j + 1]
+                    else:
+                        after = pack[i // 2] if i % 2 else pltpu.roll(pack[i // 2], 4, 0)
+                    parts.append(jnp.where(sub8, x[i, j], after))
+            at = (quad // 2 * 2 + pair) * 128 + quad % 2 * 64
+            out[at : at + 64, :] = jnp.concatenate(parts, 0).astype(BF16)
+
+    def projected(first, count):
+        at = slice(128 * first, 128 * (first + count))
+        x = x_s[at, :]
+        for part in range(3):
+            y = dot(x, wqkv[:, C * part : C * part + C]).astype(BF16)
             for g in range(GROUPS):
-                qkv_s[3 * part + g, at, :] = y[:, 128 * g : 128 * g + 128]
+                one = y[:, 128 * g : 128 * g + 128]
+                qkv_s[3 * part + g, at, :] = one
+                if part == 2:
+                    continue
+                wide = one.astype(F32)
+                square = split(wide * wide)
+                inverse = lax.rsqrt(dot(square, same) + 1.0)
+                if part == 1:
+                    kinv_s[g, at, :] = inverse
+                    continue
+                qinv_s[g, at, :] = inverse
+                across_rows = lax.rsqrt(dot(pick, square, NT) + 1.0)
+                for n in range(count):
+                    qrow_s[g, first + n, 0:PER, :] = across_rows[0:PER, 128 * n : 128 * n + 128] * scale_rows[g]
 
     head_lanes = [(lax.shift_right_logical(iota((1, 128), 1), 5) == h) for h in range(PER)]
     head_mask = [m.astype(F32).astype(BF16) for m in head_lanes]
@@ -184,6 +207,12 @@
     same = same.astype(F32).astype(BF16)
     pick = (lax.shift_right_logical(iota((8, 256), 1) & 127, 5) == iota((8, 256), 0)).astype(F32).astype(BF16)
     scales = jnp.exp(jnp.minimum(lscale[...], SCALE_CAP))
+    scale_rows = [
+        jnp.concatenate(
+            [jnp.broadcast_to(scales[:, PER * g + h : PER * g + h + 1], (1, 128)) for h in range(PER)], axis=0
+        )
+        for g in range(GROUPS)
+    ]
 
     def stacked(x):
         return jnp.concatenate([x * m for m in head_mask], axis=0)
@@ -191,35 +220,50 @@
     def across(x, h):
         return jnp.broadcast_to(x[:, 32 * h : 32 * h + 1], (128, 128))
 
+    def forward(g, pair):
+        at = slice(128 * pair, 128 * pair + 128)
+        q, k, v = qkv_s[g, at, :], qkv_s[3 + g, at, :], qkv_s[6 + g, at, :]
+        kinv = kinv_s[g, at, :]
+        raw = dot(stacked(k), q, NT)
+        low = []
+        for h in range(PER):
+            z = raw[128 * h : 128 * h + 128] * across(kinv, h) * qrow_s[g, pair, h : h + 1, :]
+            raw_s[g, pair, 128 * h : 128 * h + 128, :] = z
+            z = z + bias_s[PER * g + h] + mask_s[pair]
+            e = jnp.exp(z - jnp.max(z, axis=0, keepdims=True))
+            p = e * (1.0 / jnp.sum(e, axis=0, keepdims=True))
+            p_s[g, pair, 128 * h : 128 * h + 128, :] = p
+            low.append(p.astype(BF16))
+        att_s[g, at, :] = dot(jnp.concatenate(low, axis=0), stacked(v), TN).astype(BF16)
+
+
+    for quad in range(2):
+        shifted(quad, 0)
+    loads[3].wait()
+    projected(0, 1)
     for g in range(GROUPS):
-        scale_rows = jnp.concatenate(
-            [jnp.broadcast_to(scales[:, PER * g + h : PER * g + h + 1], (1, 128)) for h in range(PER)], axis=0
-        )
-
-        def forward(pair, carry, g=g, scale_rows=scale_rows):
-            at = pl.ds(pl.multiple_of(pair * 128, 128), 128)
-            q, k, v = qkv_s[g, at, :], qkv_s[3 + g, at, :], qkv_s[6 + g, at, :]
-            qf, kf = q.astype(F32), k.astype(F32)
-            q2, k2 = split(qf * qf), split(kf * kf)
-            qinv_s[g, at, :] = lax.rsqrt(dot(q2, same) + 1.0)
-            kinv = lax.rsqrt(dot(k2, same) + 1.0)
-            kinv_s[g, at, :] = kinv
-            qrow = lax.rsqrt(dot(pick, q2, NT) + 1.0)[0:PER] * scale_rows
-            qrow_s[g, pair, 0:PER, :] = qrow
-            raw = dot(stacked(k), q, NT)
-            low = []
-            for h in range(PER):
-                z = raw[128 * h : 128 * h + 128] * across(kinv, h) * qrow[h : h + 1]
-                raw_s[g, pair, 128 * h : 128 * h + 128, :] = z
-                z = z + bias_s[PER * g + h] + mask_s[pair]
-                e = jnp.exp(z - jnp.max(z, axis=0, keepdims=True))
-                p = e * (1.0 / jnp.sum(e, axis=0, keepdims=True))
-                p_s[g, pair, 128 * h : 128 * h + 128, :] = p
-                low.append(p.astype(BF16))
-            att_s[g, at, :] = dot(jnp.concatenate(low, axis=0), stacked(v), TN).astype(BF16)
-            return carry
-
-        lax.fori_loop(0, PAIRS, forward, 0)
+        forward(g, 0)
+
+
+    def taken(ref, send, recv):
+        pltpu.make_async_copy(ref, ref, send).wait()
+        pltpu.make_async_copy(ref, ref, recv).wait()
+
+    for n, ref in enumerate((rows_recv, pk_recv, cr_recv)):
+        taken(ref, hsem_s.at[n], hsem_r.at[n])
+
+    for quad in range(4):
+        shifted(quad, 1)
+        if quad > 1:
+            shifted(quad, 0)
+
+    projected(1, 3)
+
+    for g in range(GROUPS):
+        for pair in range(1, PAIRS):
+            forward(g, pair)
+    loads[4].wait()
+
 
     dgain = jnp.zeros((1, C), F32)
     for pair in range(PAIRS):
@@ -244,6 +288,7 @@
         sm_s[25 + g : 26 + g, :] = dgain[:, 128 * g : 128 * g + 128]
     sm_s[28:32, :] = jnp.zeros((4, 128), F32)
 
+
     att = [att_s[g] for g in range(GROUPS)]
     rows = [dot(dproj_s[...], a, TN).astype(BF16).reshape(2, 12, 16, 128) for a in att]
     for g in range(GROUPS):
@@ -254,74 +299,40 @@
     def core_copy(c):
         return remote(g_s.at[c, 1 - core], core_recv.at[c], csem_s.at[c], csem_r.at[c], (other, wa, ba))
 
-    def plane_copies(c):
-        return [
-            remote(
-                s1_s.at[c, b, w], xy_recv.at[c, d], xsem_s.at[c, d], xsem_r.at[c, d], (ha, w, b)
-            )
-            for d, (b, w) in enumerate(plane)
-        ]
-
-    def depth_copies(c):
-        return [
-            remote(z_buf.at[c, deep], z_buf.at[c, deep], zsem_s.at[c, d], zsem_r.at[c, d], (h, wa, ba))
-            for d, h in enumerate(depth)
-        ]
-
-    def level_copies(c):
-        return [
-            remote(f_s.at[c, row_mine], f_s.at[c, row_mine], fsem_s.at[c, d], fsem_r.at[c, d], (h, w, ba))
-            for d, (h, w) in enumerate(level)
-        ]
-
-    def wait_depth(c):
-        for d in range(1, 8):
-            at = (deep + 8 - d) % 8
-            copy = remote(
-                z_buf.at[c, deep], z_buf.at[c, at], zsem_s.at[c, d - 1], zsem_r.at[c, d - 1], (depth[d - 1], wa, ba)
-            )
-            copy.wait_send()
-            copy.wait_recv()
-
-    def wait_level(c):
-        for d in range(1, 16):
-            at = (row_mine + 16 - d) % 16
-            h, w = level[d - 1]
-            copy = remote(f_s.at[c, row_mine], f_s.at[c, at], fsem_s.at[c, d - 1], fsem_r.at[c, d - 1], (h, w, ba))
-            copy.wait_send()
-            copy.wait_recv()
-
-    def start_all(copies):
-        for copy in copies:
-            copy.start()
-
     def to_plane(c):
         core_copy(c).wait()
         for b in range(2):
             s1_s[c, b] = (g_s[c, core, b].astype(F32) + core_recv[c, b].astype(F32)).astype(BF16)
-        start_all(plane_copies(c))
+        for d, (b, w) in enumerate(plane):
+            remote(s1_s.at[c, b, w], xy_recv.at[c, d], xsem_s.at[c], xsem_r.at[c], (ha, w, b)).start()
 
     def to_depth(c):
-        for copy in plane_copies(c):
-            copy.wait()
+        taken(xy_recv.at[c], xsem_s.at[c], xsem_r.at[c])
         total = s1_s[c, ba, wa].astype(F32)
         for d in range(15):
             total = total + xy_recv[c, d].astype(F32)
         z_buf[c, deep] = total.astype(BF16)
-        start_all(depth_copies(c))
+        for h in depth:
+            remote(z_buf.at[c, deep], z_buf.at[c, deep], zsem_s.at[c], zsem_r.at[c], (h, wa, ba)).start()
 
     def to_level(c):
-        wait_depth(c)
+        taken(z_buf.at[c, pl.ds(0, 7)], zsem_s.at[c], zsem_r.at[c])
         total = z_buf[c, 0].astype(F32)
         for d in range(1, 8):
             total = total + z_buf[c, d].astype(F32)
         f_s[c, row_mine] = total.astype(BF16)
-        start_all(level_copies(c))
+        for h, w in level:
+            remote(f_s.at[c, row_mine], f_s.at[c, row_mine], fsem_s.at[c], fsem_r.at[c], (h, w, ba)).start()
+
+    def wait_level(c):
+        taken(f_s.at[c, pl.ds(0, 15)], fsem_s.at[c], fsem_r.at[c])
+
 
     for g in range(GROUPS):
 
-        def backward(pair, dscale, g=g):
-            at = pl.ds(pl.multiple_of(pair * 128, 128), 128)
+        dscale = jnp.zeros((PER, 128), F32)
+        for pair in range(PAIRS):
+            at = slice(128 * pair, 128 * pair + 128)
             q, k, v = qkv_s[g, at, :], qkv_s[3 + g, at, :], qkv_s[6 + g, at, :]
             datt = datt_s[g, at, :]
             qinv, kinv = qinv_s[g, at, :], kinv_s[g, at, :]
@@ -331,7 +342,10 @@
                 p = p_s[g, pair, 128 * h : 128 * h + 128, :]
                 dp = raw[128 * h : 128 * h + 128]
                 ds = p * (dp - jnp.sum(dp * p, axis=0, keepdims=True))
-                dbias_s[PER * g + h] = jnp.where(pair == 0, 0.0, dbias_s[PER * g + h]) + ds
+                if pair == 0:
+                    dbias_s[PER * g + h] = ds
+                else:
+                    dbias_s[PER * g + h] += ds
                 sums.append(jnp.sum(ds * raw_s[g, pair, 128 * h : 128 * h + 128, :], axis=0, keepdims=True))
                 grads.append((ds * across(kinv, h) * qrow_s[g, pair, h : h + 1, :]).astype(BF16))
                 low.append(p.astype(BF16))
@@ -345,9 +359,10 @@
             dqkv_s[g, at, 0:128] = dq.astype(BF16)
             dqkv_s[g, at, 128:256] = dk.astype(BF16)
             dqkv_s[g, at, 256:384] = dv.astype(BF16)
-            return dscale + jnp.concatenate(sums, axis=0)
-
-        dscale = lax.fori_loop(0, PAIRS, backward, jnp.zeros((PER, 128), F32))
+            dscale = dscale + jnp.concatenate(sums, axis=0)
+            if g > 0 and pair == 1:
+                to_plane(g - 1)
+
         here = iota((PER, 128), 0) + PER * g == iota((PER, 128), 1)
         spread = jnp.where(here, jnp.sum(dscale, axis=1, keepdims=True), 0.0)
         spread = jnp.sum(spread, axis=0, keepdims=True)
@@ -367,8 +382,7 @@
                 g_s[2, 1, 0] = keep_k[...]
                 g_s[2, 1, 1] = dw
         core_copy(g).start()
-        if g > 0:
-            to_plane(g - 1)
+
 
     sm_s[24:25, :] = scale_row
 
@@ -392,7 +406,15 @@
     )
     small_core.start()
 
+
     to_plane(2)
+
+
+    small_core.wait()
+    smx_buf[mine] = sm_s[pl.ds(pl.multiple_of(16 * core, 16), 16), :] + smc_recv[...]
+    for b, w in plane:
+        remote(smx_buf.at[mine], smx_buf.at[mine], xsem_s.at[3], xsem_r.at[3], (ha, w, b)).start()
+
 
     for pair in range(PAIRS):
         at = slice(128 * pair, 128 * pair + 128)
@@ -418,39 +440,26 @@
         tiles = [jnp.where(sub8, pltpu.roll(x[2 * i, 3], 4, 0), x[2 * i + 1, 3]) for i in range(2)]
         pk_send2[16 * quad : 16 * quad + 16, :] = jnp.concatenate(tiles, 0).astype(BF16)
     halo = [
-        remote(rows_send2, rows_recv2, hsem_s.at[6], hsem_r.at[6], (down, wa, ba)),
-        remote(pk_send2, pk_recv2, hsem_s.at[7], hsem_r.at[7], (ha, right, ba)),
-        remote(pk_send2.at[pl.ds(48, 16)], cr_recv2, hsem_s.at[8], hsem_r.at[8], (down, right, ba)),
+        remote(rows_send2, rows_recv2, hsem_s.at[3], hsem_r.at[3], (down, wa, ba)),
+        remote(pk_send2, pk_recv2, hsem_s.at[4], hsem_r.at[4], (ha, right, ba)),
+        remote(pk_send2.at[pl.ds(48, 16)], cr_recv2, hsem_s.at[5], hsem_r.at[5], (down, right, ba)),
     ]
-    start_all(halo)
-
-    small_core.wait()
-    mine16 = sm_s[pl.ds(pl.multiple_of(16 * core, 16), 16), :]
-    smx_buf[mine] = mine16 + smc_recv[...]
-    small_plane = [
-        remote(smx_buf.at[mine], smx_buf.at[mine], xsem_s.at[3, d], xsem_r.at[3, d], (ha, w, b))
-        for d, (b, w) in enumerate(plane)
-    ]
-    start_all(small_plane)
+    for copy in halo:
+        copy.start()
+
 
     for c in range(CHUNKS):
         to_depth(c)
 
-    for d in range(1, 16):
-        at = (mine + 16 - d) % 16
-        b, w = plane[d - 1]
-        copy = remote(smx_buf.at[mine], smx_buf.at[at], xsem_s.at[3, d - 1], xsem_r.at[3, d - 1], (ha, w, b))
-        copy.wait_send()
-        copy.wait_recv()
+
+    taken(smx_buf.at[pl.ds(0, 15)], xsem_s.at[3], xsem_r.at[3])
     total = smx_buf[0]
     for d in range(1, 16):
         total = total + smx_buf[d]
     smz_buf[deep] = total
-    small_depth = [
-        remote(smz_buf.at[deep], smz_buf.at[deep], zsem_s.at[3, d], zsem_r.at[3, d], (h, wa, ba))
-        for d, h in enumerate(depth)
-    ]
-    start_all(small_depth)
+    for h in depth:
+        remote(smz_buf.at[deep], smz_buf.at[deep], zsem_s.at[3], zsem_r.at[3], (h, wa, ba)).start()
+
 
     for copy in halo:
         copy.wait()
@@ -473,29 +482,24 @@
             row = 4 * quad + i
             dtok_o[0, row] = (cot[0, row].astype(F32) + back).astype(BF16)
 
+
     for c in range(CHUNKS):
         to_level(c)
 
-    for d in range(1, 8):
-        at = (deep + 8 - d) % 8
-        copy = remote(
-            smz_buf.at[deep], smz_buf.at[at], zsem_s.at[3, d - 1], zsem_r.at[3, d - 1], (depth[d - 1], wa, ba)
-        )
-        copy.wait_send()
-        copy.wait_recv()
+
+    taken(smz_buf.at[pl.ds(0, 7)], zsem_s.at[3], zsem_r.at[3])
     total = smz_buf[0]
     for d in range(1, 8):
         total = total + smz_buf[d]
     smf_buf[core] = total
-    small_last = remote(smf_buf.at[core], smf_buf.at[core], csem_s.at[4], csem_r.at[4], (other, wa, ba))
-    small_last.start()
+    remote(smf_buf.at[core], smf_buf.at[core], csem_s.at[4], csem_r.at[4], (other, wa, ba)).start()
+
 
     for c in range(CHUNKS):
         wait_level(c)
 
-    copy = remote(smf_buf.at[core], smf_buf.at[1 - core], csem_s.at[4], csem_r.at[4], (other, wa, ba))
-    copy.wait_send()
-    copy.wait_recv()
+
+    taken(smf_buf.at[0], csem_s.at[4], csem_r.at[4])
     total_o[0:16, :] = smf_buf[0]
     total_o[16:32, :] = smf_buf[1]
 
@@ -542,6 +546,11 @@
         jax.ShapeDtypeStruct((C,), F32),
     ]
     scratch = [
+        pltpu.VMEM((1, ROWS, COLS, C), BF16),
+        pltpu.VMEM((1, ROWS, COLS, C), BF16),
+        pltpu.VMEM((C, 3 * C), BF16),
+        pltpu.VMEM((C, C), BF16),
+        pltpu.VMEM((HEADS, TABLE), F32),
         pltpu.VMEM((2, 64, C), BF16),
         pltpu.VMEM((2, 4, COLS, C), BF16),
         pltpu.VMEM((2, 64, C), BF16),
@@ -578,23 +587,24 @@
         pltpu.VMEM((16, 16, 128), F32),
         pltpu.VMEM((8, 16, 128), F32),
         pltpu.VMEM((2, 16, 128), F32),
-        pltpu.SemaphoreType.DMA((9,)),
-        pltpu.SemaphoreType.DMA((9,)),
+        pltpu.SemaphoreType.DMA((5,)),
+        pltpu.SemaphoreType.DMA((6,)),
+        pltpu.SemaphoreType.DMA((6,)),
         pltpu.SemaphoreType.DMA((5,)),
         pltpu.SemaphoreType.DMA((5,)),
-        pltpu.SemaphoreType.DMA((4, 15)),
-        pltpu.SemaphoreType.DMA((4, 15)),
-        pltpu.SemaphoreType.DMA((4, 7)),
-        pltpu.SemaphoreType.DMA((4, 7)),
-        pltpu.SemaphoreType.DMA((3, 15)),
-        pltpu.SemaphoreType.DMA((3, 15)),
+        pltpu.SemaphoreType.DMA((4,)),
+        pltpu.SemaphoreType.DMA((4,)),
+        pltpu.SemaphoreType.DMA((4,)),
+        pltpu.SemaphoreType.DMA((4,)),
+        pltpu.SemaphoreType.DMA((3,)),
+        pltpu.SemaphoreType.DMA((3,)),
     ]
     lscale = logit_scale.reshape(1, HEADS)
     moved, pieces, total = pl.pallas_call(
         kernel,
         name="window_backward",
         out_shape=middle,
-        in_specs=[vmem] * 7,
+        in_specs=[pl.BlockSpec(memory_space=pl.ANY)] * 5 + [vmem] * 2,
         out_specs=[vmem] * 3,
         scratch_shapes=scratch,
         compiler_params=pltpu.CompilerParams(collective_id=0, has_side_effects=True),

time: 64.2 us -> 54.8 us (0.85)
  Pallas kernels: 63.4 us -> 54 us
    pallas_call x1, Pallas kernels: 60.8 us -> 51.3 us  [step(): pl.pallas_call(kernel, name='window_backward', out_shape=middle, in_specs...]
where the time goes in v2:
time: 54.8 us; the launch traced here: 54.6 us
  Pallas kernels  54 us (99%)
  between operations  0.64 us (1%)
    pallas_call x1, Pallas kernels, step(): pl.pallas_call(kernel, name='window_backward', out_shape=middle, in_specs...  51.3 us
    pallas_call x1, Pallas kernels, step(): pl.pallas_call(finish, name='finish', out_shape=outs, in_specs=[vmem] * 5...  2.63 us

profile of v2, /device:TPU:1, one launch (start us, length us, event | category | flops | bytes accessed | tf_op | source)
XLA Modules:
  0.0 54.6 jit_solution(12053275020641144789)
XLA Ops:
  0.6 51.3 %window_backward.1 = (bf16[1,16,32,384]{3,2,1,0:T(8,128)(2,1)}, bf16[3,16,16,384]{3,2,1,0:T(8,128)(2,1)}, f32[32,128]{1,0:T(8,128)}) custom-call(bf16[1,16,32,384]{3,2,1,0:T(8,128)(2,1)} %tok_h.1, bf16[1,16,32,384]{3,2,1,0:T(8,128)(2,1)} %cot_h.1, bf16[384,1152]{1,0:T(8,128)(2,1)} %wqkv_h.1, bf16[384,384]{1,0:T(8,128)(2,1)} %wproj_h.1, f32[12,225]{1,0:T(8,128)} %table.1, ...), custom_call_target="tpu_custom_call" | custom-call | tf_op jit(solution)/shard_map/window_backward/pallas_call | solution.py:603
  52.0 2.6 %finish.1 = (bf16[1,16,32,384]{3,2,1,0:T(8,128)(2,1)}, f32[576,384]{1,0:T(8,128)}, f32[192,384]{1,0:T(8,128)}, f32[12,225]{1,0:T(8,128)}, f32[1,12]{1,0:T(1,128)}, /*index=5*/f32[384]{0:T(512)}) custom-call(bf16[3,16,16,384]{3,2,1,0:T(8,128)(2,1)} %get-tuple-element.15.pieces, f32[32,128]{1,0:T(8,128)} %get-tuple-element.16.total, ...), custom_call_target="tpu_custom_call" | custom-call | tf_op jit(solution)/shard_map/finish/pallas_call | solution.py:612

commit v3 on v2

--- a/solution.py
+++ b/solution.py
@@ -27,7 +27,7 @@
 PAIRS = 4
 TABLE = 225
 CHUNKS = 3
-BARRIER = 34
+BARRIER = 7
 
 NT = (((1,), (1,)), ((), ()))
 TN = (((0,), (0,)), ((), ()))
@@ -68,20 +68,23 @@
 
 
 def kernel(
-    tok_h, cot_h, wqkv_h, wproj_h, table_h, lscale, gain,
-    dtok_o, f_s, total_o,
-    tok, cot, wqkv, wproj, table,
+    tok_h, cot_h, wqkv_h, wproj_h, table_h, lscale_h, gain_h,
+    dtok_o, f_s, total_o, factor_o,
+    tok, cot, wqkv, wproj, table, lscale, gain,
     pk_send, rows_recv, pk_recv, cr_recv,
     x_s, c_s, qkv_s, qinv_s, kinv_s, qrow_s, bias_s, mask_s, p_s, raw_s, att_s, datt_s, dproj_s, dqkv_s, dbias_s, dm_s,
     rows_send2, pk_send2, rows_recv2, pk_recv2, cr_recv2,
     keep_k, g_s, core_recv, s1_s, xy_recv, z_buf,
     sm_s, smc_recv, smx_buf, smz_buf, smf_buf,
-    lsem, hsem_s, hsem_r, csem_s, csem_r, xsem_s, xsem_r, zsem_s, zsem_r, fsem_s, fsem_r,
+    told, lsem, hsem_s, hsem_r, csem_s, csem_r, xsem_s, xsem_r, zsem_s, zsem_r, fsem_s, fsem_r,
 ):
     loads = [
         pltpu.make_async_copy(src, dst, lsem.at[n])
         for n, (src, dst) in enumerate(
-            ((tok_h, tok), (cot_h, cot), (table_h, table), (wqkv_h, wqkv), (wproj_h, wproj))
+            (
+                (tok_h, tok), (cot_h, cot), (table_h, table), (wqkv_h, wqkv), (wproj_h, wproj),
+                (lscale_h, lscale), (gain_h, gain),
+            )
         )
     ]
     for load in loads:
@@ -107,10 +110,7 @@
         level.append((deep * 2 + at // 8, at % 8))
 
     barrier = pltpu.get_barrier_semaphore()
-    greeted = [(other, wa, ba)]
-    greeted += [(ha, w, b) for b, w in plane]
-    greeted += [(h, wa, ba) for h in depth]
-    greeted += [(other, (wa + d) % 8, ba) for d in range(1, 8)]
+    greeted = [(ha, left, ba), (ha, right, ba), (ha, wa, 1 - ba)]
     greeted += [(up, wa, ba), (down, wa, ba), (up, left, ba), (down, right, ba)]
     for device in greeted:
         pl.semaphore_signal(barrier, inc=1, device_id=device, device_id_type=MESH)
@@ -128,9 +128,13 @@
 
 
     loads[2].wait()
+    loads[5].wait()
+    loads[6].wait()
     onehot = offset_onehot()
     sigma = jax.nn.sigmoid(table[...])
     lanes = fine(sigma * BIAS_RANGE, onehot)
+    factor_o[0:HEADS, 0:TABLE] = BIAS_RANGE * sigma * (1.0 - sigma)
+    factor_o[HEADS : HEADS + 1, 0:HEADS] = (lscale[...] < SCALE_CAP).astype(F32)
     for h in range(HEADS):
         line = jnp.broadcast_to(lanes[h : h + 1, :], (128, 256))
         bias_s[h] = pltpu.roll(line, 0, 1, stride=1, stride_axis=0)[:, :128]
@@ -155,12 +159,17 @@
 
     pl.semaphore_wait(barrier, BARRIER)
     for n, ref in enumerate((tok, cot)):
-        remote(ref.at[0, pl.ds(0, 4)], rows_recv.at[n], hsem_s.at[0], hsem_r.at[0], (up, wa, ba)).start()
-        remote(pk_send.at[n], pk_recv.at[n], hsem_s.at[1], hsem_r.at[1], (ha, left, ba)).start()
-        remote(pk_send.at[n, pl.ds(0, 16)], cr_recv.at[n], hsem_s.at[2], hsem_r.at[2], (up, left, ba)).start()
-
-    def shifted(quad, pair):
-        for n, (ref, out) in enumerate(((tok, x_s), (cot, c_s))):
+        for m, (src, dst, device) in enumerate(
+            (
+                (ref.at[0, pl.ds(0, 4)], rows_recv.at[n], (up, wa, ba)),
+                (pk_send.at[n], pk_recv.at[n], (ha, left, ba)),
+                (pk_send.at[n, pl.ds(0, 16)], cr_recv.at[n], (up, left, ba)),
+            )
+        ):
+            remote(src, dst, hsem_s.at[3 * n + m], hsem_r.at[3 * n + m], device).start()
+
+    def shifted(n, quad, pair):
+        for ref, out in (((tok, x_s), (cot, c_s))[n],):
             if quad < 3:
                 rows = ref[0, 4 * quad + 4 : 4 * quad + 8]
             else:
@@ -236,9 +245,15 @@
             low.append(p.astype(BF16))
         att_s[g, at, :] = dot(jnp.concatenate(low, axis=0), stacked(v), TN).astype(BF16)
 
+    def tell(n, devices):
+        for device in devices:
+            pl.semaphore_signal(told.at[n], inc=1, device_id=device, device_id_type=MESH)
+
+    tell(0, [(ha, left, ba), (ha, right, ba), (up, wa, ba), (down, wa, ba)])
+
 
     for quad in range(2):
-        shifted(quad, 0)
+        shifted(0, quad, 0)
     loads[3].wait()
     projected(0, 1)
     for g in range(GROUPS):
@@ -249,13 +264,15 @@
         pltpu.make_async_copy(ref, ref, send).wait()
         pltpu.make_async_copy(ref, ref, recv).wait()
 
-    for n, ref in enumerate((rows_recv, pk_recv, cr_recv)):
-        taken(ref, hsem_s.at[n], hsem_r.at[n])
+    for m, ref in enumerate((rows_recv, pk_recv, cr_recv)):
+        taken(ref.at[0], hsem_s.at[m], hsem_r.at[m])
+    pl.semaphore_wait(told.at[0], 4)
+    tell(1, [(ha, (wa + 2) % 8, ba), (ha, (wa + 6) % 8, ba), ((ha + 2) % 16, wa, ba), ((ha + 14) % 16, wa, ba)])
 
     for quad in range(4):
-        shifted(quad, 1)
+        shifted(0, quad, 1)
         if quad > 1:
-            shifted(quad, 0)
+            shifted(0, quad, 0)
 
     projected(1, 3)
 
@@ -263,6 +280,14 @@
         for pair in range(1, PAIRS):
             forward(g, pair)
     loads[4].wait()
+
+    for m, ref in enumerate((rows_recv, pk_recv, cr_recv)):
+        taken(ref.at[1], hsem_s.at[3 + m], hsem_r.at[3 + m])
+    pl.semaphore_wait(told.at[1], 4)
+    tell(2, [(ha, wa, 1 - ba), (other, wa, ba), ((ha + 4) % 16, wa, ba), ((ha + 12) % 16, wa, ba)])
+    for quad in range(4):
+        for pair in range(2):
+            shifted(1, quad, pair)
 
 
     dgain = jnp.zeros((1, C), F32)
@@ -361,6 +386,8 @@
             dqkv_s[g, at, 256:384] = dv.astype(BF16)
             dscale = dscale + jnp.concatenate(sums, axis=0)
             if g > 0 and pair == 1:
+                if g == 1:
+                    pl.semaphore_wait(told.at[2], 4)
                 to_plane(g - 1)
 
         here = iota((PER, 128), 0) + PER * g == iota((PER, 128), 1)
@@ -440,9 +467,9 @@
         tiles = [jnp.where(sub8, pltpu.roll(x[2 * i, 3], 4, 0), x[2 * i + 1, 3]) for i in range(2)]
         pk_send2[16 * quad : 16 * quad + 16, :] = jnp.concatenate(tiles, 0).astype(BF16)
     halo = [
-        remote(rows_send2, rows_recv2, hsem_s.at[3], hsem_r.at[3], (down, wa, ba)),
-        remote(pk_send2, pk_recv2, hsem_s.at[4], hsem_r.at[4], (ha, right, ba)),
-        remote(pk_send2.at[pl.ds(48, 16)], cr_recv2, hsem_s.at[5], hsem_r.at[5], (down, right, ba)),
+        remote(rows_send2, rows_recv2, hsem_s.at[6], hsem_r.at[6], (down, wa, ba)),
+        remote(pk_send2, pk_recv2, hsem_s.at[7], hsem_r.at[7], (ha, right, ba)),
+        remote(pk_send2.at[pl.ds(48, 16)], cr_recv2, hsem_s.at[8], hsem_r.at[8], (down, right, ba)),
     ]
     for copy in halo:
         copy.start()
@@ -504,7 +531,7 @@
     total_o[16:32, :] = smf_buf[1]
 
 
-def finish(pieces, total, moved, table, lscale, dtok_o, dwqkv_o, dwproj_o, dtable_o, dscale_o, dgain_o):
+def finish(pieces, total, moved, factor, dtok_o, dwqkv_o, dwproj_o, dtable_o, dscale_o, dgain_o):
     ba = lax.axis_index("ba")
     dtok_o[...] = moved[...]
 
@@ -522,10 +549,8 @@
     dwqkv_o[rows(384 - 320 * ba, 128), :] = join(2, 1, 0, 8)
 
     by_lane = jnp.concatenate([total[0:12], total[12:24]], axis=1)
-    sigma = jax.nn.sigmoid(table[...])
-    dtable_o[...] = fine(by_lane, offset_onehot(), NT) * (BIAS_RANGE * sigma * (1.0 - sigma))
-    live = (lscale[...] < SCALE_CAP).astype(F32)
-    dscale_o[...] = total[24:25, 0:HEADS] * live
+    dtable_o[...] = fine(by_lane, offset_onehot(), NT) * factor[0:HEADS, 0:TABLE]
+    dscale_o[...] = total[24:25, 0:HEADS] * factor[HEADS : HEADS + 1, 0:HEADS]
     for g in range(GROUPS):
         dgain_o[pl.ds(128 * g, 128)] = total[25 + g]
 
@@ -533,9 +558,10 @@
 def step(tokens, cotangent, w_qkv, w_proj, table_logits, logit_scale, gain):
     vmem = pl.BlockSpec(memory_space=pltpu.VMEM)
     middle = [
-        jax.ShapeDtypeStruct((1, ROWS, COLS, C), BF16),
-        jax.ShapeDtypeStruct((CHUNKS, 16, 16, C), BF16),
-        jax.ShapeDtypeStruct((32, 128), F32),
+        pltpu.VMEM((1, ROWS, COLS, C), BF16),
+        pltpu.VMEM((CHUNKS, 16, 16, C), BF16),
+        pltpu.VMEM((32, 128), F32),
+        pltpu.VMEM((16, 256), F32),
     ]
     outs = [
         jax.ShapeDtypeStruct((1, ROWS, COLS, C), BF16),
@@ -551,6 +577,8 @@
         pltpu.VMEM((C, 3 * C), BF16),
         pltpu.VMEM((C, C), BF16),
         pltpu.VMEM((HEADS, TABLE), F32),
+        pltpu.VMEM((1, HEADS), F32),
+        pltpu.VMEM((C,), F32),
         pltpu.VMEM((2, 64, C), BF16),
         pltpu.VMEM((2, 4, COLS, C), BF16),
         pltpu.VMEM((2, 64, C), BF16),
@@ -587,9 +615,10 @@
         pltpu.VMEM((16, 16, 128), F32),
         pltpu.VMEM((8, 16, 128), F32),
         pltpu.VMEM((2, 16, 128), F32),
-        pltpu.SemaphoreType.DMA((5,)),
-        pltpu.SemaphoreType.DMA((6,)),
-        pltpu.SemaphoreType.DMA((6,)),
+        pltpu.SemaphoreType.REGULAR((3,)),
+        pltpu.SemaphoreType.DMA((7,)),
+        pltpu.SemaphoreType.DMA((9,)),
+        pltpu.SemaphoreType.DMA((9,)),
         pltpu.SemaphoreType.DMA((5,)),
         pltpu.SemaphoreType.DMA((5,)),
         pltpu.SemaphoreType.DMA((4,)),
@@ -600,18 +629,18 @@
         pltpu.SemaphoreType.DMA((3,)),
     ]
     lscale = logit_scale.reshape(1, HEADS)
-    moved, pieces, total = pl.pallas_call(
+    moved, pieces, total, factor = pl.pallas_call(
         kernel,
         name="window_backward",
         out_shape=middle,
-        in_specs=[pl.BlockSpec(memory_space=pl.ANY)] * 5 + [vmem] * 2,
-        out_specs=[vmem] * 3,
+        in_specs=[pl.BlockSpec(memory_space=pltpu.HBM)] * 7,
+        out_specs=[vmem] * 4,
         scratch_shapes=scratch,
-        compiler_params=pltpu.CompilerParams(collective_id=0, has_side_effects=True),
+        compiler_params=pltpu.CompilerParams(collective_id=0, has_side_effects=True, vmem_limit_bytes=65_980_000),
     )(tokens, cotangent, w_qkv, w_proj, table_logits, lscale, gain)
     d_tokens, d_wqkv, d_wproj, d_table, d_scale, d_gain = pl.pallas_call(
-        finish, name="finish", out_shape=outs, in_specs=[vmem] * 5, out_specs=[vmem] * 6
-    )(pieces, total, moved, table_logits, lscale)
+        finish, name="finish", out_shape=outs, in_specs=[vmem] * 4, out_specs=[vmem] * 6, compiler_params=pltpu.CompilerParams(vmem_limit_bytes=16 * 2**20)
+    )(pieces, total, moved, factor)
     return d_tokens, d_wqkv.T, d_wproj.T, d_table, d_scale.reshape(HEADS), d_gain
 
 

time: 54.8 us -> 51.1 us (0.932)
  Pallas kernels: 54 us -> 50.3 us
    pallas_call x1, Pallas kernels: 51.3 us -> 48.9 us  [step(): pl.pallas_call(kernel, name='window_backward', out_shape=middle, in_specs...]
    pallas_call x1, Pallas kernels: 2.63 us -> 1.42 us  [step(): pl.pallas_call(finish, name='finish', out_shape=outs, in_specs=[vmem] * 4...]
where the time goes in v3:
time: 51.1 us; the launch traced here: 51 us
  Pallas kernels  50.3 us (98%)
  between operations  0.64 us (1%)
    pallas_call x1, Pallas kernels, step(): pl.pallas_call(kernel, name='window_backward', out_shape=middle, in_specs...  48.9 us
    pallas_call x1, Pallas kernels, step(): pl.pallas_call(finish, name='finish', out_shape=outs, in_specs=[vmem] * 4...  1.42 us

profile of v3, /device:TPU:1, one launch (start us, length us, event | category | flops | bytes accessed | tf_op | source)
XLA Modules:
  0.0 51.0 jit_solution(11795977402771776825)
XLA Ops:
  0.6 48.9 %window_backward.1 = (bf16[1,16,32,384]{3,2,1,0:T(8,128)(2,1)S(1)}, bf16[3,16,16,384]{3,2,1,0:T(8,128)(2,1)S(1)}, f32[32,128]{1,0:T(8,128)S(1)}, f32[16,256]{1,0:T(8,128)S(1)}) custom-call(bf16[1,16,32,384]{3,2,1,0:T(8,128)(2,1)} %tok_h.1, bf16[1,16,32,384]{3,2,1,0:T(8,128)(2,1)} %cot_h.1, bf16[384,1152]{1,0:T(8,128)(2,1)} %wqkv_h.1, ...), custom_call_target="tpu_custom_call" | custom-call | tf_op jit(solution)/shard_map/window_backward/pallas_call | solution.py:632
  49.6 1.4 %finish.1 = (bf16[1,16,32,384]{3,2,1,0:T(8,128)(2,1)}, f32[576,384]{1,0:T(8,128)}, f32[192,384]{1,0:T(8,128)}, f32[12,225]{1,0:T(8,128)}, f32[1,12]{1,0:T(1,128)}, /*index=5*/f32[384]{0:T(512)}) custom-call(bf16[3,16,16,384]{3,2,1,0:T(8,128)(2,1)S(1)} %get-tuple-element.16.pieces, f32[32,128]{1,0:T(8,128)S(1)} %get-tuple-element.17.total, ...), custom_call_target="tpu_custom_call" | custom-call | tf_op jit(solution)/shard_map/finish/pallas_call | solution.py:641

commit v4 on v3

--- a/solution.py
+++ b/solution.py
@@ -15,7 +15,6 @@
 
 EPS_NORM = 1e-05
 MASK_FILL = -100.0
-OTHER_WINDOW = -1e30
 SCALE_CAP = math.log(100.0)
 BIAS_RANGE = 16.0
 
@@ -55,9 +54,9 @@
 def offset_onehot():
     entry = iota((TABLE, 256), 0)
     row = lax.shift_right_logical(entry * 4370, 16)
-    col = entry - 15 * row
-    lane = (row - 7) * 16 + (col - 7)
-    lane = jnp.where(lane < 0, lane + 256, lane)
+    col = entry - 15 * row - 7
+    lane = ((row - 7) * 8 + col) & 127
+    lane = jnp.where(col < 0, lane + 128, lane)
     return (lane == iota((TABLE, 256), 1)).astype(F32)
 
 
@@ -72,7 +71,7 @@
     dtok_o, f_s, total_o, factor_o,
     tok, cot, wqkv, wproj, table, lscale, gain,
     pk_send, rows_recv, pk_recv, cr_recv,
-    x_s, c_s, qkv_s, qinv_s, kinv_s, qrow_s, bias_s, mask_s, p_s, raw_s, att_s, datt_s, dproj_s, dqkv_s, dbias_s, dm_s,
+    x_s, c_s, qkv_s, qinv_s, kinv_s, qrow_s, bias_s, mask_s, p_s, raw_s, both_s, att_s, datt_s, dproj_s, dqkv_s, dbias_s, dm_s,
     rows_send2, pk_send2, rows_recv2, pk_recv2, cr_recv2,
     keep_k, g_s, core_recv, s1_s, xy_recv, z_buf,
     sm_s, smc_recv, smx_buf, smz_buf, smf_buf,
@@ -87,7 +86,7 @@
             )
         )
     ]
-    for load in loads:
+    for load in loads[0:2]:
         load.start()
 
     ha, wa, ba = lax.axis_index("ha"), lax.axis_index("wa"), lax.axis_index("ba")
@@ -120,41 +119,13 @@
 
     loads[0].wait()
     loads[1].wait()
+    for load in loads[2:]:
+        load.start()
     for n, ref in enumerate((tok, cot)):
         for quad in range(4):
             x = ref[0, 4 * quad : 4 * quad + 4, 0:16, :].astype(F32).reshape(4, 2, 8, C)[:, 0]
             tiles = [jnp.where(sub8, x[2 * i], pltpu.roll(x[2 * i + 1], 4, 0)) for i in range(2)]
             pk_send[n, 16 * quad : 16 * quad + 16, :] = jnp.concatenate(tiles, 0).astype(BF16)
-
-
-    loads[2].wait()
-    loads[5].wait()
-    loads[6].wait()
-    onehot = offset_onehot()
-    sigma = jax.nn.sigmoid(table[...])
-    lanes = fine(sigma * BIAS_RANGE, onehot)
-    factor_o[0:HEADS, 0:TABLE] = BIAS_RANGE * sigma * (1.0 - sigma)
-    factor_o[HEADS : HEADS + 1, 0:HEADS] = (lscale[...] < SCALE_CAP).astype(F32)
-    for h in range(HEADS):
-        line = jnp.broadcast_to(lanes[h : h + 1, :], (128, 256))
-        bias_s[h] = pltpu.roll(line, 0, 1, stride=1, stride_axis=0)[:, :128]
-    key, query = iota((128, 128), 0), iota((128, 128), 1)
-
-    def bit(x, n):
-        return lax.shift_right_logical(x, n) & 1
-
-    apart = bit(key, 3) != bit(query, 3)
-    low_rows = bit(key, 6) != bit(query, 6)
-    low_cols = bit(key, 2) != bit(query, 2)
-    second = bit(key, 3) == 1
-    for pair in range(PAIRS):
-        differ = jnp.zeros((128, 128), jnp.int32)
-        if pair // 2 == 1:
-            differ = jnp.where(low_rows, (ha == 15).astype(jnp.int32), differ)
-        if pair % 2 == 1:
-            differ = jnp.maximum(differ, jnp.where(low_cols & second, (wa == 7).astype(jnp.int32), 0))
-        value = jnp.where(differ > 0, MASK_FILL, 0.0).astype(F32)
-        mask_s[pair] = jnp.where(apart, OTHER_WINDOW, value)
 
 
     pl.semaphore_wait(barrier, BARRIER)
@@ -178,16 +149,17 @@
             if pair == 1:
                 pack = pk_recv[n, 16 * quad + 16 : 16 * quad + 32, :] if quad < 3 else cr_recv[n]
                 pack = pack.astype(F32).reshape(2, 8, C)
-            parts = []
-            for i in range(4):
-                for j in (2 * pair, 2 * pair + 1):
+            for window in range(2):
+                j = 2 * pair + window
+                parts = []
+                for i in range(4):
                     if j < 3:
                         after = x[i, j + 1]
                     else:
                         after = pack[i // 2] if i % 2 else pltpu.roll(pack[i // 2], 4, 0)
                     parts.append(jnp.where(sub8, x[i, j], after))
-            at = (quad // 2 * 2 + pair) * 128 + quad % 2 * 64
-            out[at : at + 64, :] = jnp.concatenate(parts, 0).astype(BF16)
+                at = (quad // 2 * 2 + pair) * 128 + window * 64 + quad % 2 * 32
+                out[at : at + 32, :] = jnp.concatenate(parts, 0).astype(BF16)
 
     def projected(first, count):
         at = slice(128 * first, 128 * (first + count))
@@ -212,9 +184,14 @@
 
     head_lanes = [(lax.shift_right_logical(iota((1, 128), 1), 5) == h) for h in range(PER)]
     head_mask = [m.astype(F32).astype(BF16) for m in head_lanes]
+    head_mask2 = [jnp.concatenate([m, m], axis=1) for m in head_mask]
+    left_lanes = (iota((1, 128), 1) < 64).astype(F32).astype(BF16)
+    right_lanes = (iota((1, 128), 1) >= 64).astype(F32).astype(BF16)
     same = (lax.shift_right_logical(iota((256, 128), 0) & 127, 5) == lax.shift_right_logical(iota((256, 128), 1), 5))
     same = same.astype(F32).astype(BF16)
     pick = (lax.shift_right_logical(iota((8, 256), 1) & 127, 5) == iota((8, 256), 0)).astype(F32).astype(BF16)
+    for n in (2, 5, 6):
+        loads[n].wait()
     scales = jnp.exp(jnp.minimum(lscale[...], SCALE_CAP))
     scale_rows = [
         jnp.concatenate(
@@ -226,59 +203,121 @@
     def stacked(x):
         return jnp.concatenate([x * m for m in head_mask], axis=0)
 
+    def paired(x):
+        wide = jnp.concatenate([x[0:64], x[64:128]], axis=1)
+        return jnp.concatenate([wide * m for m in head_mask2], axis=0)
+
+    def apart(x):
+        none = jnp.zeros((64, 128), BF16)
+        return jnp.concatenate(
+            [jnp.concatenate([x[0:64], none], axis=1), jnp.concatenate([none, x[64:128]], axis=1)], axis=0
+        )
+
+    def own(x):
+        return jnp.concatenate([x[0:64, 0:128], x[64:128, 128:256]], axis=0)
+
+    def spread(x):
+        return jnp.concatenate([x * left_lanes, x * right_lanes], axis=0)
+
     def across(x, h):
-        return jnp.broadcast_to(x[:, 32 * h : 32 * h + 1], (128, 128))
-
-    def forward(g, pair):
-        at = slice(128 * pair, 128 * pair + 128)
-        q, k, v = qkv_s[g, at, :], qkv_s[3 + g, at, :], qkv_s[6 + g, at, :]
-        kinv = kinv_s[g, at, :]
-        raw = dot(stacked(k), q, NT)
-        low = []
-        for h in range(PER):
-            z = raw[128 * h : 128 * h + 128] * across(kinv, h) * qrow_s[g, pair, h : h + 1, :]
-            raw_s[g, pair, 128 * h : 128 * h + 128, :] = z
-            z = z + bias_s[PER * g + h] + mask_s[pair]
-            e = jnp.exp(z - jnp.max(z, axis=0, keepdims=True))
-            p = e * (1.0 / jnp.sum(e, axis=0, keepdims=True))
-            p_s[g, pair, 128 * h : 128 * h + 128, :] = p
-            low.append(p.astype(BF16))
-        att_s[g, at, :] = dot(jnp.concatenate(low, axis=0), stacked(v), TN).astype(BF16)
+        return jnp.where(
+            query < 64,
+            jnp.broadcast_to(x[0:64, 32 * h : 32 * h + 1], (64, 128)),
+            jnp.broadcast_to(x[64:128, 32 * h : 32 * h + 1], (64, 128)),
+        )
+
+    def forward(items):
+        raws = []
+        for g, pair in items:
+            at = slice(128 * pair, 128 * pair + 128)
+            raws.append(dot(paired(qkv_s[3 + g, at, :]), apart(qkv_s[g, at, :]), NT))
+        lows = []
+        for (g, pair), raw in zip(items, raws):
+            kinv = kinv_s[g, 128 * pair : 128 * pair + 128, :]
+            low = []
+            for h in range(PER):
+                rows = slice(64 * h, 64 * h + 64)
+                both = across(kinv, h) * qrow_s[g, pair, h : h + 1, :]
+                both_s[g, pair, rows, :] = both
+                z = raw[rows] * both
+                raw_s[g, pair, rows, :] = z
+                z = z + bias_s[PER * g + h] + mask_s[pair]
+                e = jnp.exp(z - jnp.max(z, axis=0, keepdims=True))
+                p = e * (1.0 / jnp.sum(e, axis=0, keepdims=True))
+                p_s[g, pair, rows, :] = p
+                low.append(p.astype(BF16))
+            lows.append(low)
+        for (g, pair), low in zip(items, lows):
+            at = slice(128 * pair, 128 * pair + 128)
+            v = paired(qkv_s[6 + g, at, :])
+            att_s[g, at, :] = own(dot(jnp.concatenate(low, axis=0), v, TN)).astype(BF16)
 
     def tell(n, devices):
         for device in devices:
             pl.semaphore_signal(told.at[n], inc=1, device_id=device, device_id_type=MESH)
 
     tell(0, [(ha, left, ba), (ha, right, ba), (up, wa, ba), (down, wa, ba)])
+
+
+    onehot = offset_onehot()
+    sigma = jax.nn.sigmoid(table[...])
+    lanes = fine(sigma * BIAS_RANGE, onehot)
+    factor_o[0:HEADS, 0:TABLE] = BIAS_RANGE * sigma * (1.0 - sigma)
+    factor_o[HEADS : HEADS + 1, 0:HEADS] = (lscale[...] < SCALE_CAP).astype(F32)
+    key, query = iota((64, 128), 0), iota((64, 128), 1)
+    first = query < 64
+    ahead = (query & 7) >= (key & 7)
+
+    def bit(x, n):
+        return lax.shift_right_logical(x, n) & 1
+
+    for h in range(HEADS):
+        turned = [
+            pltpu.roll(jnp.broadcast_to(lanes[h : h + 1, at : at + 128], (64, 128)), 0, 1, stride=1, stride_axis=0)
+            for at in (0, 128)
+        ]
+        one = jnp.where(ahead, turned[0], turned[1])
+        bias_s[h] = jnp.where(first, one, pltpu.roll(one, 64, 1))
+    low_rows = bit(key, 5) != bit(query, 5)
+    low_cols = bit(key, 2) != bit(query, 2)
+    for pair in range(PAIRS):
+        differ = jnp.zeros((64, 128), jnp.int32)
+        if pair // 2 == 1:
+            differ = jnp.where(low_rows, (ha == 15).astype(jnp.int32), differ)
+        if pair % 2 == 1:
+            differ = jnp.maximum(differ, jnp.where(low_cols & (query >= 64), (wa == 7).astype(jnp.int32), 0))
+        mask_s[pair] = jnp.where(differ > 0, MASK_FILL, 0.0).astype(F32)
 
 
     for quad in range(2):
         shifted(0, quad, 0)
     loads[3].wait()
     projected(0, 1)
-    for g in range(GROUPS):
-        forward(g, 0)
+    forward([(g, 0) for g in range(GROUPS)])
 
 
     def taken(ref, send, recv):
         pltpu.make_async_copy(ref, ref, send).wait()
         pltpu.make_async_copy(ref, ref, recv).wait()
 
-    for m, ref in enumerate((rows_recv, pk_recv, cr_recv)):
-        taken(ref.at[0], hsem_s.at[m], hsem_r.at[m])
+    taken(pk_recv.at[0], hsem_s.at[1], hsem_r.at[1])
+
+    for quad in range(2):
+        shifted(0, quad, 1)
+    projected(1, 1)
+    forward([(g, 1) for g in range(GROUPS)])
+
+    taken(rows_recv.at[0], hsem_s.at[0], hsem_r.at[0])
+    taken(cr_recv.at[0], hsem_s.at[2], hsem_r.at[2])
     pl.semaphore_wait(told.at[0], 4)
     tell(1, [(ha, (wa + 2) % 8, ba), (ha, (wa + 6) % 8, ba), ((ha + 2) % 16, wa, ba), ((ha + 14) % 16, wa, ba)])
 
-    for quad in range(4):
-        shifted(0, quad, 1)
-        if quad > 1:
-            shifted(0, quad, 0)
-
-    projected(1, 3)
-
-    for g in range(GROUPS):
-        for pair in range(1, PAIRS):
-            forward(g, pair)
+    for quad in range(2, 4):
+        for pair in range(2):
+            shifted(0, quad, pair)
+    projected(2, 2)
+
+    forward([(g, pair) for g in range(GROUPS) for pair in range(2, PAIRS)])
     loads[4].wait()
 
     for m, ref in enumerate((rows_recv, pk_recv, cr_recv)):
@@ -290,23 +329,25 @@
             shifted(1, quad, pair)
 
 
+    def mean(x):
+        return jnp.mean(x, -1, keepdims=True)
+
+    spans = [slice(128 * pair, 128 * pair + 128) for pair in range(PAIRS)]
+    proj = [dot(jnp.concatenate([att_s[g, at, :] for g in range(GROUPS)], axis=1), wproj[...]) for at in spans]
+    upstream = [c_s[at, :].astype(F32) for at in spans]
+    scaled = [x * gain[...].reshape(1, C) for x in upstream]
+    centre = [x - m for x, m in zip(proj, [mean(x) for x in proj])]
+    scaled = [x - m for x, m in zip(scaled, [mean(x) for x in scaled])]
+    inv_std = [lax.rsqrt(m + EPS_NORM) for m in [mean(x * x) for x in centre]]
+    normed = [x * r for x, r in zip(centre, inv_std)]
+    along = [mean(x * (u * gain[...].reshape(1, C))) for x, u in zip(normed, upstream)]
+    dproj = [(r * (u - x * m)).astype(BF16) for r, u, x, m in zip(inv_std, scaled, normed, along)]
     dgain = jnp.zeros((1, C), F32)
-    for pair in range(PAIRS):
-        at = slice(128 * pair, 128 * pair + 128)
-        att = jnp.concatenate([att_s[g, at, :] for g in range(GROUPS)], axis=1)
-        proj = dot(att, wproj[...])
-        centre = proj - jnp.mean(proj, -1, keepdims=True)
-        inv_std = lax.rsqrt(jnp.mean(centre * centre, -1, keepdims=True) + EPS_NORM)
-        normed = centre * inv_std
-        upstream = c_s[at, :].astype(F32)
-        dgain = dgain + jnp.sum(upstream * normed, 0, keepdims=True)
-        scaled = upstream * gain[...].reshape(1, C)
-        dproj = inv_std * (
-            scaled - jnp.mean(scaled, -1, keepdims=True) - normed * jnp.mean(scaled * normed, -1, keepdims=True)
-        )
-        dproj = dproj.astype(BF16)
-        dproj_s[at, :] = dproj
-        datt = dot(dproj, wproj[...], NT).astype(BF16)
+    for u, x in zip(upstream, normed):
+        dgain = dgain + jnp.sum(u * x, 0, keepdims=True)
+    for at, d in zip(spans, dproj):
+        dproj_s[at, :] = d
+        datt = dot(d, wproj[...], NT).astype(BF16)
         for g in range(GROUPS):
             datt_s[g, at, :] = datt[:, 128 * g : 128 * g + 128]
     for g in range(GROUPS):
@@ -356,44 +397,49 @@
     for g in range(GROUPS):
 
         dscale = jnp.zeros((PER, 128), F32)
-        for pair in range(PAIRS):
-            at = slice(128 * pair, 128 * pair + 128)
-            q, k, v = qkv_s[g, at, :], qkv_s[3 + g, at, :], qkv_s[6 + g, at, :]
-            datt = datt_s[g, at, :]
-            qinv, kinv = qinv_s[g, at, :], kinv_s[g, at, :]
-            raw = dot(stacked(v), datt, NT)
-            low, grads, sums = [], [], []
+        spans = [slice(128 * pair, 128 * pair + 128) for pair in range(PAIRS)]
+        raws = [dot(paired(qkv_s[6 + g, at, :]), apart(datt_s[g, at, :]), NT) for at in spans]
+        lows, grads = [], []
+        for pair, raw in enumerate(raws):
+            low, grad, sums = [], [], []
             for h in range(PER):
-                p = p_s[g, pair, 128 * h : 128 * h + 128, :]
-                dp = raw[128 * h : 128 * h + 128]
+                rows = slice(64 * h, 64 * h + 64)
+                p = p_s[g, pair, rows, :]
+                dp = raw[rows]
                 ds = p * (dp - jnp.sum(dp * p, axis=0, keepdims=True))
                 if pair == 0:
                     dbias_s[PER * g + h] = ds
                 else:
                     dbias_s[PER * g + h] += ds
-                sums.append(jnp.sum(ds * raw_s[g, pair, 128 * h : 128 * h + 128, :], axis=0, keepdims=True))
-                grads.append((ds * across(kinv, h) * qrow_s[g, pair, h : h + 1, :]).astype(BF16))
+                sums.append(jnp.sum(ds * raw_s[g, pair, rows, :], axis=0, keepdims=True))
+                grad.append((ds * both_s[g, pair, rows, :]).astype(BF16))
                 low.append(p.astype(BF16))
-            dv = dot(jnp.concatenate(low, axis=1), stacked(datt))
-            a = dot(jnp.concatenate(grads, axis=0), stacked(k), TN)
-            b = dot(jnp.concatenate(grads, axis=1), stacked(q))
-            qf, kf = q.astype(F32), k.astype(F32)
-            uq, uk = qf * qinv, kf * kinv
-            dq = a - uq * dot(split(uq * a), same)
-            dk = b - uk * dot(split(uk * b), same)
-            dqkv_s[g, at, 0:128] = dq.astype(BF16)
-            dqkv_s[g, at, 128:256] = dk.astype(BF16)
+            dscale = dscale + jnp.concatenate(sums, axis=0)
+            lows.append(low)
+            grads.append(grad)
+        if g > 0:
+            if g == 1:
+                pl.semaphore_wait(told.at[2], 4)
+            to_plane(g - 1)
+        a = [
+            own(dot(jnp.concatenate(grad, axis=0), paired(qkv_s[3 + g, at, :]), TN)) for grad, at in zip(grads, spans)
+        ]
+        b = [
+            dot(jnp.concatenate([spread(x) for x in grad], axis=1), stacked(qkv_s[g, at, :]))
+            for grad, at in zip(grads, spans)
+        ]
+        for low, at in zip(lows, spans):
+            dv = dot(jnp.concatenate([spread(x) for x in low], axis=1), stacked(datt_s[g, at, :]))
             dqkv_s[g, at, 256:384] = dv.astype(BF16)
-            dscale = dscale + jnp.concatenate(sums, axis=0)
-            if g > 0 and pair == 1:
-                if g == 1:
-                    pl.semaphore_wait(told.at[2], 4)
-                to_plane(g - 1)
-
+        for part, (grad, inverse) in enumerate(((a, qinv_s), (b, kinv_s))):
+            unit = [qkv_s[3 * part + g, at, :].astype(F32) * inverse[g, at, :] for at in spans]
+            along = [dot(split(u * x), same) for u, x in zip(unit, grad)]
+            for u, x, y, at in zip(unit, grad, along, spans):
+                dqkv_s[g, at, 128 * part : 128 * part + 128] = (x - u * y).astype(BF16)
         here = iota((PER, 128), 0) + PER * g == iota((PER, 128), 1)
-        spread = jnp.where(here, jnp.sum(dscale, axis=1, keepdims=True), 0.0)
-        spread = jnp.sum(spread, axis=0, keepdims=True)
-        scale_row = spread if g == 0 else scale_row + spread
+        placed = jnp.where(here, jnp.sum(dscale, axis=1, keepdims=True), 0.0)
+        placed = jnp.sum(placed, axis=0, keepdims=True)
+        scale_row = placed if g == 0 else scale_row + placed
         for part in range(3):
             dw = dot(dqkv_s[g, :, 128 * part : 128 * part + 128], x_s[...], TN).astype(BF16).reshape(8, 16, C)
             if part == 0:
@@ -413,21 +459,17 @@
 
     sm_s[24:25, :] = scale_row
 
-    lane8, sub256 = iota((8, 128), 1), iota((8, 256), 0)
+    sub128 = iota((8, 128), 0)
     for h in range(HEADS):
-        ahead = dbias_s[h, 0:8, :]
-        behind = jnp.zeros((8, 128), F32)
-        for n in range(1, 16):
-            turned = pltpu.roll(dbias_s[h, 8 * n : 8 * n + 8, :], 128 - 8 * n, 1)
-            inside = lane8 < 128 - 8 * n
-            ahead = ahead + jnp.where(inside, turned, 0.0)
-            behind = behind + jnp.where(inside, 0.0, turned)
-        both = jnp.concatenate([ahead, behind], axis=1)
-        for n in range(3):
-            both = jnp.where(bit(sub256, n) == 1, pltpu.roll(both, 256 - 2**n, 1), both)
-        both = jnp.sum(both, axis=0, keepdims=True)
-        sm_s[h : h + 1, :] = both[:, 0:128]
-        sm_s[12 + h : 13 + h, :] = both[:, 128:256]
+        both = dbias_s[h]
+        both = jnp.where(first, both + pltpu.roll(both, 64, 1), 0.0)
+        for m, part in enumerate((jnp.where(ahead, both, 0.0), jnp.where(ahead, 0.0, both))):
+            total = part[0:8]
+            for n in range(1, 8):
+                total = total + pltpu.roll(part[8 * n : 8 * n + 8], 128 - 8 * n, 1)
+            for n in range(3):
+                total = jnp.where(bit(sub128, n) == 1, pltpu.roll(total, 128 - 2**n, 1), total)
+            sm_s[12 * m + h : 12 * m + h + 1, :] = jnp.sum(total, axis=0, keepdims=True)
     small_core = remote(
         sm_s.at[pl.ds(pl.multiple_of(16 * (1 - core), 16), 16)], smc_recv, csem_s.at[3], csem_r.at[3], (other, wa, ba)
     )
@@ -441,6 +483,9 @@
     smx_buf[mine] = sm_s[pl.ds(pl.multiple_of(16 * core, 16), 16), :] + smc_recv[...]
     for b, w in plane:
         remote(smx_buf.at[mine], smx_buf.at[mine], xsem_s.at[3], xsem_r.at[3], (ha, w, b)).start()
+
+
+    to_depth(0)
 
 
     for pair in range(PAIRS):
@@ -449,21 +494,22 @@
         for g in range(GROUPS):
             w = jnp.concatenate([wqkv[:, C * n + 128 * g : C * n + 128 * g + 128] for n in range(3)], axis=1)
             total = total + dot(dqkv_s[g, at, :], w, NT)
-        dm_s[at, :] = total.astype(BF16)
+        dm_s[at, :] = total.astype(BF16).astype(F32)
 
     def image_rows(quad):
         parts = []
         for i in range(4):
             for pair in range(2):
-                at = (quad // 2 * 2 + pair) * 128 + quad % 2 * 64 + 16 * i
-                parts.append(dm_s[at : at + 16, :])
-        return jnp.concatenate(parts, axis=0).reshape(4, 32, C)
+                for window in range(2):
+                    at = (quad // 2 * 2 + pair) * 128 + window * 64 + quad % 2 * 32 + 8 * i
+                    parts.append(dm_s[at : at + 8, :])
+        return jnp.concatenate(parts, axis=0)
 
     for quad in range(4):
         x = image_rows(quad)
         if quad == 3:
-            rows_send2[...] = x
-        x = x.astype(F32).reshape(4, 4, 8, C)
+            rows_send2[...] = x.astype(BF16).reshape(4, COLS, C)
+        x = x.reshape(4, 4, 8, C)
         tiles = [jnp.where(sub8, pltpu.roll(x[2 * i, 3], 4, 0), x[2 * i + 1, 3]) for i in range(2)]
         pk_send2[16 * quad : 16 * quad + 16, :] = jnp.concatenate(tiles, 0).astype(BF16)
     halo = [
@@ -475,8 +521,10 @@
         copy.start()
 
 
-    for c in range(CHUNKS):
-        to_depth(c)
+    to_depth(1)
+    to_depth(2)
+    to_level(0)
+    to_level(1)
 
 
     taken(smx_buf.at[pl.ds(0, 15)], xsem_s.at[3], xsem_r.at[3])
@@ -488,14 +536,25 @@
         remote(smz_buf.at[deep], smz_buf.at[deep], zsem_s.at[3], zsem_r.at[3], (h, wa, ba)).start()
 
 
+    to_level(2)
+
+
+    taken(smz_buf.at[pl.ds(0, 7)], zsem_s.at[3], zsem_r.at[3])
+    total = smz_buf[0]
+    for d in range(1, 8):
+        total = total + smz_buf[d]
+    smf_buf[core] = total
+    remote(smf_buf.at[core], smf_buf.at[core], csem_s.at[4], csem_r.at[4], (other, wa, ba)).start()
+
+
     for copy in halo:
         copy.wait()
     for quad in range(4):
         if quad == 0:
-            rows, pack = rows_recv2[...], cr_recv2[...]
+            rows, pack = rows_recv2[...].astype(F32), cr_recv2[...]
         else:
             rows, pack = image_rows(quad - 1), pk_recv2[16 * quad - 16 : 16 * quad, :]
-        x = pltpu.roll(rows.astype(F32).reshape(16, 8, C), 4, 1).reshape(4, 4, 8, C)
+        x = pltpu.roll(rows.reshape(16, 8, C), 4, 1).reshape(4, 4, 8, C)
         pack = pack.astype(F32).reshape(2, 8, C)
         for i in range(4):
             parts = []
@@ -508,18 +567,6 @@
             back = jnp.concatenate(parts, 0)
             row = 4 * quad + i
             dtok_o[0, row] = (cot[0, row].astype(F32) + back).astype(BF16)
-
-
-    for c in range(CHUNKS):
-        to_level(c)
-
-
-    taken(smz_buf.at[pl.ds(0, 7)], zsem_s.at[3], zsem_r.at[3])
-    total = smz_buf[0]
-    for d in range(1, 8):
-        total = total + smz_buf[d]
-    smf_buf[core] = total
-    remote(smf_buf.at[core], smf_buf.at[core], csem_s.at[4], csem_r.at[4], (other, wa, ba)).start()
 
 
     for c in range(CHUNKS):
@@ -589,16 +636,17 @@
         pltpu.VMEM((GROUPS, TOKENS, 128), F32),
         pltpu.VMEM((GROUPS, TOKENS, 128), F32),
         pltpu.VMEM((GROUPS, PAIRS, 8, 128), F32),
-        pltpu.VMEM((HEADS, 128, 128), F32),
-        pltpu.VMEM((PAIRS, 128, 128), F32),
-        pltpu.VMEM((GROUPS, PAIRS, TOKENS, 128), F32),
-        pltpu.VMEM((GROUPS, PAIRS, TOKENS, 128), F32),
+        pltpu.VMEM((HEADS, 64, 128), F32),
+        pltpu.VMEM((PAIRS, 64, 128), F32),
+        pltpu.VMEM((GROUPS, PAIRS, 256, 128), F32),
+        pltpu.VMEM((GROUPS, PAIRS, 256, 128), F32),
+        pltpu.VMEM((GROUPS, PAIRS, 256, 128), F32),
         pltpu.VMEM((GROUPS, TOKENS, 128), BF16),
         pltpu.VMEM((GROUPS, TOKENS, 128), BF16),
         pltpu.VMEM((TOKENS, C), BF16),
         pltpu.VMEM((GROUPS, TOKENS, C), BF16),
-        pltpu.VMEM((HEADS, 128, 128), F32),
-        pltpu.VMEM((TOKENS, C), BF16),
+        pltpu.VMEM((HEADS, 64, 128), F32),
+        pltpu.VMEM((TOKENS, C), F32),
         pltpu.VMEM((4, COLS, C), BF16),
         pltpu.VMEM((64, C), BF16),
         pltpu.VMEM((4, COLS, C), BF16),

time: 51.1 us -> 45.8 us (0.90)
  Pallas kernels: 50.3 us -> 45 us
    pallas_call x1, Pallas kernels: 48.9 us -> 43.5 us  [step(): pl.pallas_call(kernel, name='window_backward', out_shape=middle, in_specs...]
where the time goes in v4:
time: 45.8 us; the launch traced here: 45.6 us
  Pallas kernels  45 us (98%)
  between operations  0.64 us (1%)
    pallas_call x1, Pallas kernels, step(): pl.pallas_call(kernel, name='window_backward', out_shape=middle, in_specs...  43.5 us
    pallas_call x1, Pallas kernels, step(): pl.pallas_call(finish, name='finish', out_shape=outs, in_specs=[vmem] * 4...  1.42 us

profile of v4, /device:TPU:1, one launch (start us, length us, event | category | flops | bytes accessed | tf_op | source)
XLA Modules:
  0.0 45.6 jit_solution(4410974128554832671)
XLA Ops:
  0.6 43.5 %window_backward.1 = (bf16[1,16,32,384]{3,2,1,0:T(8,128)(2,1)S(1)}, bf16[3,16,16,384]{3,2,1,0:T(8,128)(2,1)S(1)}, f32[32,128]{1,0:T(8,128)S(1)}, f32[16,256]{1,0:T(8,128)S(1)}) custom-call(bf16[1,16,32,384]{3,2,1,0:T(8,128)(2,1)} %tok_h.1, bf16[1,16,32,384]{3,2,1,0:T(8,128)(2,1)} %cot_h.1, bf16[384,1152]{1,0:T(8,128)(2,1)} %wqkv_h.1, ...), custom_call_target="tpu_custom_call" | custom-call | tf_op jit(solution)/shard_map/window_backward/pallas_call | solution.py:680
  44.2 1.4 %finish.1 = (bf16[1,16,32,384]{3,2,1,0:T(8,128)(2,1)}, f32[576,384]{1,0:T(8,128)}, f32[192,384]{1,0:T(8,128)}, f32[12,225]{1,0:T(8,128)}, f32[1,12]{1,0:T(1,128)}, /*index=5*/f32[384]{0:T(512)}) custom-call(bf16[3,16,16,384]{3,2,1,0:T(8,128)(2,1)S(1)} %get-tuple-element.16.pieces, f32[32,128]{1,0:T(8,128)S(1)} %get-tuple-element.17.total, ...), custom_call_target="tpu_custom_call" | custom-call | tf_op jit(solution)/shard_map/finish/pallas_call | solution.py:689

commit v5 on v4

--- a/solution.py
+++ b/solution.py
@@ -74,7 +74,7 @@
     x_s, c_s, qkv_s, qinv_s, kinv_s, qrow_s, bias_s, mask_s, p_s, raw_s, both_s, att_s, datt_s, dproj_s, dqkv_s, dbias_s, dm_s,
     rows_send2, pk_send2, rows_recv2, pk_recv2, cr_recv2,
     keep_k, g_s, core_recv, s1_s, xy_recv, z_buf,
-    sm_s, smc_recv, smx_buf, smz_buf, smf_buf,
+    sm_s, smc_recv, smy_buf, smx_buf, smz_buf, smf_buf,
     told, lsem, hsem_s, hsem_r, csem_s, csem_r, xsem_s, xsem_r, zsem_s, zsem_r, fsem_s, fsem_r,
 ):
     loads = [
@@ -98,15 +98,17 @@
     mine = ba * 8 + wa
     row_mine = core * 8 + wa
 
-    plane = []
-    for d in range(1, 16):
-        at = (mine + d) % 16
-        plane.append((at // 8, at % 8))
-    depth = [(deep + d) % 8 * 2 + core for d in range(1, 8)]
-    level = []
-    for d in range(1, 16):
-        at = (row_mine + d) % 16
-        level.append((deep * 2 + at // 8, at % 8))
+    high, low_x = wa // 2, wa % 2
+
+    def seat(a, b, c):
+        return (ba + a) % 2, (high + b) % 4 * 2 + (low_x + c) % 2
+
+    hops = {(a, b, c): (0, 1, 2, 1)[b] + (0, 1, 2, 1)[2 * a + c] for a in range(2) for b in range(4) for c in range(2)}
+    away = sorted((o for o in hops if hops[o]), key=lambda o: (-hops[o], o))
+    plane = [seat(*o) for o in away]
+    depth = [(deep + d) % 8 * 2 + core for d in (4, 3, 5, 2, 6, 1, 7)]
+    rows_away = [seat(*o)[1] for o in away if o[0] == 0]
+    level = [[(ha, w) for w in rows_away], [(other, w) for w in rows_away] + [(ha, w) for w in rows_away] + [(other, wa)]]
 
     barrier = pltpu.get_barrier_semaphore()
     greeted = [(ha, left, ba), (ha, right, ba), (ha, wa, 1 - ba)]
@@ -387,11 +389,19 @@
         for d in range(1, 8):
             total = total + z_buf[c, d].astype(F32)
         f_s[c, row_mine] = total.astype(BF16)
-        for h, w in level:
+        for h, w in level[c // 2]:
             remote(f_s.at[c, row_mine], f_s.at[c, row_mine], fsem_s.at[c], fsem_r.at[c], (h, w, ba)).start()
 
+    def to_core(c):
+        taken(f_s.at[c, pl.ds(0, 7)], fsem_s.at[c], fsem_r.at[c])
+        half = f_s.at[c, pl.ds(pl.multiple_of(8 * core, 8), 8)]
+        remote(half, half, csem_s.at[5 + c], csem_r.at[5 + c], (other, wa, ba)).start()
+
     def wait_level(c):
-        taken(f_s.at[c, pl.ds(0, 15)], fsem_s.at[c], fsem_r.at[c])
+        if c < 2:
+            taken(f_s.at[c, pl.ds(0, 8)], csem_s.at[5 + c], csem_r.at[5 + c])
+        else:
+            taken(f_s.at[c, pl.ds(0, 15)], fsem_s.at[c], fsem_r.at[c])
 
 
     for g in range(GROUPS):
@@ -480,9 +490,9 @@
 
 
     small_core.wait()
-    smx_buf[mine] = sm_s[pl.ds(pl.multiple_of(16 * core, 16), 16), :] + smc_recv[...]
-    for b, w in plane:
-        remote(smx_buf.at[mine], smx_buf.at[mine], xsem_s.at[3], xsem_r.at[3], (ha, w, b)).start()
+    smy_buf[high] = sm_s[pl.ds(pl.multiple_of(16 * core, 16), 16), :] + smc_recv[...]
+    for b in (2, 1, 3):
+        remote(smy_buf.at[high], smy_buf.at[high], xsem_s.at[3], xsem_r.at[3], (ha, seat(0, b, 0)[1], ba)).start()
 
 
     to_depth(0)
@@ -522,21 +532,32 @@
 
 
     to_depth(1)
+
+    column = 2 * ba + low_x
+    taken(smy_buf.at[pl.ds(0, 3)], xsem_s.at[3], xsem_r.at[3])
+    smx_buf[column] = smy_buf[0] + smy_buf[1] + smy_buf[2] + smy_buf[3]
+    for a, c in ((1, 0), (0, 1), (1, 1)):
+        b, w = seat(a, 0, c)
+        remote(smx_buf.at[column], smx_buf.at[column], xsem_s.at[4], xsem_r.at[4], (ha, w, b)).start()
+
+    to_level(0)
+
     to_depth(2)
-    to_level(0)
+
     to_level(1)
 
 
-    taken(smx_buf.at[pl.ds(0, 15)], xsem_s.at[3], xsem_r.at[3])
-    total = smx_buf[0]
-    for d in range(1, 16):
-        total = total + smx_buf[d]
-    smz_buf[deep] = total
+    taken(smx_buf.at[pl.ds(0, 3)], xsem_s.at[4], xsem_r.at[4])
+    smz_buf[deep] = smx_buf[0] + smx_buf[1] + smx_buf[2] + smx_buf[3]
     for h in depth:
         remote(smz_buf.at[deep], smz_buf.at[deep], zsem_s.at[3], zsem_r.at[3], (h, wa, ba)).start()
 
+    to_core(0)
+
 
     to_level(2)
+
+    to_core(1)
 
 
     taken(smz_buf.at[pl.ds(0, 7)], zsem_s.at[3], zsem_r.at[3])
@@ -660,17 +681,18 @@
         pltpu.VMEM((CHUNKS, 8, 16, C), BF16),
         pltpu.VMEM((32, 128), F32),
         pltpu.VMEM((16, 128), F32),
-        pltpu.VMEM((16, 16, 128), F32),
+        pltpu.VMEM((4, 16, 128), F32),
+        pltpu.VMEM((4, 16, 128), F32),
         pltpu.VMEM((8, 16, 128), F32),
         pltpu.VMEM((2, 16, 128), F32),
         pltpu.SemaphoreType.REGULAR((3,)),
         pltpu.SemaphoreType.DMA((7,)),
         pltpu.SemaphoreType.DMA((9,)),
         pltpu.SemaphoreType.DMA((9,)),
+        pltpu.SemaphoreType.DMA((7,)),
+        pltpu.SemaphoreType.DMA((7,)),
         pltpu.SemaphoreType.DMA((5,)),
         pltpu.SemaphoreType.DMA((5,)),
-        pltpu.SemaphoreType.DMA((4,)),
-        pltpu.SemaphoreType.DMA((4,)),
         pltpu.SemaphoreType.DMA((4,)),
         pltpu.SemaphoreType.DMA((4,)),
         pltpu.SemaphoreType.DMA((3,)),

time: 45.8 us -> 43.7 us (0.954)
  Pallas kernels: 45 us -> 42.9 us
    pallas_call x1, Pallas kernels: 43.5 us -> 41.4 us  [step(): pl.pallas_call(kernel, name='window_backward', out_shape=middle, in_specs...]
where the time goes in v5:
time: 43.7 us; the launch traced here: 43.5 us
  Pallas kernels  42.9 us (98%)
  between operations  0.64 us (1%)
    pallas_call x1, Pallas kernels, step(): pl.pallas_call(kernel, name='window_backward', out_shape=middle, in_specs...  41.4 us
    pallas_call x1, Pallas kernels, step(): pl.pallas_call(finish, name='finish', out_shape=outs, in_specs=[vmem] * 4...  1.42 us

profile of v5, /device:TPU:1, one launch (start us, length us, event | category | flops | bytes accessed | tf_op | source)
XLA Modules:
  0.0 43.5 jit_solution(14496558988859971417)
XLA Ops:
  0.6 41.4 %window_backward.1 = (bf16[1,16,32,384]{3,2,1,0:T(8,128)(2,1)S(1)}, bf16[3,16,16,384]{3,2,1,0:T(8,128)(2,1)S(1)}, f32[32,128]{1,0:T(8,128)S(1)}, f32[16,256]{1,0:T(8,128)S(1)}) custom-call(bf16[1,16,32,384]{3,2,1,0:T(8,128)(2,1)} %tok_h.1, bf16[1,16,32,384]{3,2,1,0:T(8,128)(2,1)} %cot_h.1, bf16[384,1152]{1,0:T(8,128)(2,1)} %wqkv_h.1, ...), custom_call_target="tpu_custom_call" | custom-call | tf_op jit(solution)/shard_map/window_backward/pallas_call | solution.py:702
  42.1 1.4 %finish.1 = (bf16[1,16,32,384]{3,2,1,0:T(8,128)(2,1)}, f32[576,384]{1,0:T(8,128)}, f32[192,384]{1,0:T(8,128)}, f32[12,225]{1,0:T(8,128)}, f32[1,12]{1,0:T(1,128)}, /*index=5*/f32[384]{0:T(512)}) custom-call(bf16[3,16,16,384]{3,2,1,0:T(8,128)(2,1)S(1)} %get-tuple-element.16.pieces, f32[32,128]{1,0:T(8,128)S(1)} %get-tuple-element.17.total, ...), custom_call_target="tpu_custom_call" | custom-call | tf_op jit(solution)/shard_map/finish/pallas_call | solution.py:711

commit v6 on v5

--- a/solution.py
+++ b/solution.py
@@ -540,17 +540,16 @@
         b, w = seat(a, 0, c)
         remote(smx_buf.at[column], smx_buf.at[column], xsem_s.at[4], xsem_r.at[4], (ha, w, b)).start()
 
+    to_depth(2)
+
     to_level(0)
-
-    to_depth(2)
-
-    to_level(1)
-
 
     taken(smx_buf.at[pl.ds(0, 3)], xsem_s.at[4], xsem_r.at[4])
     smz_buf[deep] = smx_buf[0] + smx_buf[1] + smx_buf[2] + smx_buf[3]
     for h in depth:
         remote(smz_buf.at[deep], smz_buf.at[deep], zsem_s.at[3], zsem_r.at[3], (h, wa, ba)).start()
+
+    to_level(1)
 
     to_core(0)
 

time: 43.7 us -> 44.4 us (1.016)
  Pallas kernels: 42.9 us -> 43.6 us
    pallas_call x1, Pallas kernels: 41.4 us -> 42.2 us  [step(): pl.pallas_call(kernel, name='window_backward', out_shape=middle, in_specs...]
where the time goes in v6:
time: 44.4 us; the launch traced here: 44.3 us
  Pallas kernels  43.6 us (98%)
  between operations  0.64 us (1%)
    pallas_call x1, Pallas kernels, step(): pl.pallas_call(kernel, name='window_backward', out_shape=middle, in_specs...  42.2 us
    pallas_call x1, Pallas kernels, step(): pl.pallas_call(finish, name='finish', out_shape=outs, in_specs=[vmem] * 4...  1.42 us

profile of v6, /device:TPU:1, one launch (start us, length us, event | category | flops | bytes accessed | tf_op | source)
XLA Modules:
  0.0 44.3 jit_solution(8556397491271881814)
XLA Ops:
  0.6 42.2 %window_backward.1 = (bf16[1,16,32,384]{3,2,1,0:T(8,128)(2,1)S(1)}, bf16[3,16,16,384]{3,2,1,0:T(8,128)(2,1)S(1)}, f32[32,128]{1,0:T(8,128)S(1)}, f32[16,256]{1,0:T(8,128)S(1)}) custom-call(bf16[1,16,32,384]{3,2,1,0:T(8,128)(2,1)} %tok_h.1, bf16[1,16,32,384]{3,2,1,0:T(8,128)(2,1)} %cot_h.1, bf16[384,1152]{1,0:T(8,128)(2,1)} %wqkv_h.1, ...), custom_call_target="tpu_custom_call" | custom-call | tf_op jit(solution)/shard_map/window_backward/pallas_call | solution.py:701
  42.9 1.4 %finish.1 = (bf16[1,16,32,384]{3,2,1,0:T(8,128)(2,1)}, f32[576,384]{1,0:T(8,128)}, f32[192,384]{1,0:T(8,128)}, f32[12,225]{1,0:T(8,128)}, f32[1,12]{1,0:T(1,128)}, /*index=5*/f32[384]{0:T(512)}) custom-call(bf16[3,16,16,384]{3,2,1,0:T(8,128)(2,1)S(1)} %get-tuple-element.16.pieces, f32[32,128]{1,0:T(8,128)S(1)} %get-tuple-element.17.total, ...), custom_call_target="tpu_custom_call" | custom-call | tf_op jit(solution)/shard_map/finish/pallas_call | solution.py:710
